TPU v7x, 512 devices: a 8x2x16 block of a 8x8x16 slice. The times are simulated.
512 devices in a mesh: member: 2 (over y), gx: 16 (over x, core), gy: 16 (over z).
Axes of the slice: x: 8, y: 2, z: 16, core: 2. Of those that a mesh axis runs over, the one named last changes fastest.
The devices are a block of a 8x8x16 slice.
Arguments:
- perm: float32 [64, 128, 2048], P('member', 'gx', 'gy'), parts along dimension 0, may hold values from 0.2 to 5
- facies: int32 [64, 128, 2048], P('member', 'gx', 'gy'), parts along dimension 0, may hold values from 0 to 3
- facies_porosity: float32 [4], replicated, may hold values from 0.15 to 0.35
- facies_mobility: float32 [4], replicated, may hold values from 0.5 to 2
- pressure: float32 [64, 128, 2048], P('member', 'gx', 'gy'), parts along dimension 0, may hold values from -6 to 6
- saturation: float32 [64, 128, 2048], P('member', 'gx', 'gy'), parts along dimension 0, may hold values from 0.1 to 0.9
- basis: float32 [64, 128, 2048], P('member', 'gx', 'gy'), parts along dimension 0, may hold values from 0.75 to 1.33
- bx_map: int32 [256], P('member'), parts along dimension 0, may hold values from 0 to 15, as said below
- by_map: int32 [4096], P('member'), parts along dimension 0, may hold values from 0 to 255, as said below
- well_cells: int32 [1024], P('member'), parts along dimension 0, may hold values from 0 to 262143
- well_rates: float32 [1024], P('member'), parts along dimension 0, may hold values from -384 to 384
Outputs:
- new_pressure: float32 [64, 128, 2048], P('member', 'gx', 'gy'), parts along dimension 0
- new_saturation: float32 [64, 128, 2048], P('member', 'gx', 'gy'), parts along dimension 0
There are 2 independent parts, one for each index of `member`. A program takes and returns all parts, laid end to end along the dimension named above; an argument that names none is the same for every part. Nothing has to cross between parts.
Inputs may be any that keep to these rules, and one draw needn't show every extreme that they name: `bx_map`: never falling; block 0 begins at position 0 and block k >= 1 begins at position 8 k + d with -2 <= d <= 2. `by_map`: never falling; block 0 begins at position 0 and block k >= 1 begins at position 8 k + d with -2 <= d <= 2.
All inputs are finite; a program needn't handle non-finite values.
Results may differ from a plain program's by a relative error of at most 0.0003.
Values sent between devices are 32-bit elements; how exact they have to be, the bound alone decides.
A program may use at most 64 MiB of HBM per device.

v0:
```python
import jax
import jax.numpy as jnp
from jax import lax
from jax.sharding import PartitionSpec as P

NZ = 32
BX = 8
BY = 8
BZ = 4
NSWEEP = 3
NSUB = 4
NFAC = 4


viscosity_ratio = 4.0
vertical_factor = 0.1
storage_coefficient = 0.5
relaxation = 0.5
time_step = 0.005
highest = lax.Precision.HIGHEST


def padded(block, sides, width):
    for axis, dim in sides:
        count = lax.axis_size(axis)
        forward = [(i, i + 1) for i in range(count - 1)]
        backward = [(target, source) for source, target in forward]
        low = lax.ppermute(
            lax.slice_in_dim(block, block.shape[dim] - width, None, axis=dim), axis, forward
        )
        high = lax.ppermute(lax.slice_in_dim(block, 0, width, axis=dim), axis, backward)
        block = jnp.concatenate([low, block, high], axis=dim)
    return block


def with_halo(array, sides, width):
    edges = {}
    for axis, dim in sides:
        size, length = (lax.axis_size(axis), array.shape[dim])
        up = [(i, (i + 1) % size) for i in range(size - 1)]
        last = lax.slice_in_dim(array, length - width, length, axis=dim)
        first = lax.slice_in_dim(array, 0, width, axis=dim)
        edges[dim] = (
            lax.ppermute(last, axis, up),
            lax.ppermute(first, axis, [(b, a) for a, b in up]),
        )
    done = []
    for _, dim in sides:
        low, high = edges[dim]
        around = [(width, width) if d in done else (0, 0) for d in range(array.ndim)]
        array = jnp.concatenate([jnp.pad(low, around), array, jnp.pad(high, around)], axis=dim)
        done.append(dim)
    return array


def lower(field, axis):
    return lax.slice_in_dim(field, 0, field.shape[axis] - 1, axis=axis)


def upper(field, axis):
    return lax.slice_in_dim(field, 1, field.shape[axis], axis=axis)


def pad_after(field, axis):
    widths = [(0, 1) if position == axis else (0, 0) for position in range(field.ndim)]
    return jnp.pad(field, widths)


def pad_before(field, axis):
    widths = [(1, 0) if position == axis else (0, 0) for position in range(field.ndim)]
    return jnp.pad(field, widths)


def trim_border(field, border_width):
    if border_width == 0:
        return field
    return field[
        :,
        border_width : field.shape[1] - border_width,
        border_width : field.shape[2] - border_width,
    ]


def split_layers(stacked, count):
    height = stacked.shape[0] // count
    return tuple(
        (stacked[height * position : height * (position + 1)] for position in range(count))
    )


def harmonic(left, right):
    total = left + right
    return 2.0 * left * right / jnp.where(total > 0, total, 1.0)


def total_mobility(water_saturation):
    return (
        water_saturation * water_saturation
        + (1.0 - water_saturation) * (1.0 - water_saturation) / viscosity_ratio
    )


def fractional(water_saturation):
    wet = water_saturation * water_saturation
    return wet / (wet + (1.0 - water_saturation) * (1.0 - water_saturation) / viscosity_ratio)


def transmissibilities(mobility):
    return tuple(
        (
            (vertical_factor if axis == 0 else 1.0)
            * harmonic(lower(mobility, axis), upper(mobility, axis))
            for axis in range(3)
        )
    )


def outflow(flows):
    total = 0.0
    for axis in range(3):
        total = total + pad_after(flows[axis], axis) - pad_before(flows[axis], axis)
    return total


def lookup(indices, table):
    total = jnp.zeros(indices.shape, jnp.float32)
    for level in range(NFAC):
        total = total + jnp.where(indices == level, table[level], 0.0)
    return total


def relax(wide_estimate, system):
    resid_c, diag_c, pos_z, neg_z, pos_x, neg_x, pos_y, neg_y = system
    center = wide_estimate[:, 1:-1, 1:-1]
    applied = diag_c * center
    applied = (
        applied - pos_z * pad_after(upper(center, 0), 0) - neg_z * pad_before(lower(center, 0), 0)
    )
    applied = applied - pos_x * wide_estimate[:, 2:, 1:-1] - neg_x * wide_estimate[:, :-2, 1:-1]
    applied = applied - pos_y * wide_estimate[:, 1:-1, 2:] - neg_y * wide_estimate[:, 1:-1, :-2]
    return center + relaxation * (resid_c - applied) / diag_c


def march_forward(water_saturation, flows, source, porosity):
    frac = fractional(water_saturation)
    carried = tuple(
        (
            jnp.where(flows[axis] > 0, lower(frac, axis), upper(frac, axis)) * flows[axis]
            for axis in range(3)
        )
    )
    change = jnp.maximum(source, 0.0) + jnp.minimum(source, 0.0) * frac - outflow(carried)
    return trim_border(water_saturation + time_step / porosity * change, 1)


def body(
    perm,
    facies,
    facies_porosity,
    facies_mobility,
    pressure,
    saturation,
    basis,
    bx_map,
    by_map,
    well_cells,
    well_rates,
):
    layers, width_x, width_y = pressure.shape
    blocks_x = width_x // BX
    blocks_y = width_y // BY
    index_x = lax.axis_index("gx")
    index_y = lax.axis_index("gy")
    porosity = lookup(facies, facies_porosity)
    mobility = perm * lookup(facies, facies_mobility) * total_mobility(saturation)
    border_width = NSUB
    stacked = jnp.concatenate((pressure, mobility, basis, porosity, saturation), axis=0)
    widened = padded(stacked, (("gx", 1), ("gy", 2)), NSUB)
    extended_pressure, extended_mobility, extended_basis, extended_porosity, ext_water = (
        split_layers(widened, 5)
    )
    span_x = width_x + 2 * border_width
    span_y = width_y + 2 * border_width
    cells_x = index_x * width_x - border_width + jnp.arange(span_x, dtype=jnp.int32)
    cells_y = index_y * width_y - border_width + jnp.arange(span_y, dtype=jnp.int32)
    map_x = lax.dynamic_slice_in_dim(
        jnp.pad(bx_map, (border_width, border_width), constant_values=-1), index_x * width_x, span_x
    )
    map_y = lax.dynamic_slice_in_dim(
        jnp.pad(by_map, (border_width, border_width), constant_values=-1), index_y * width_y, span_y
    )
    full_y = by_map.shape[0]
    well_x = well_cells // full_y
    well_y = well_cells % full_y
    hits_x = jnp.where(well_x[:, None] == cells_x[None, :], well_rates[:, None], 0.0)
    hits_y = (well_y[:, None] == cells_y[None, :]).astype(jnp.float32)
    column = jnp.einsum("wa,wb->ab", hits_x, hits_y, precision=highest) / NZ
    source = jnp.broadcast_to(column[None], (layers, span_x, span_y))
    trans = transmissibilities(extended_mobility)
    pushes = tuple(
        (
            trans[axis] * (lower(extended_pressure, axis) - upper(extended_pressure, axis))
            for axis in range(3)
        )
    )
    residual = source - outflow(pushes)
    conductance = 0.0
    for axis in range(3):
        conductance = conductance + pad_after(trans[axis], axis) + pad_before(trans[axis], axis)
    cell_diagonal = (
        extended_basis * extended_basis * (storage_coefficient * extended_porosity + conductance)
    )
    layer_blocks = jnp.arange(layers, dtype=jnp.int32) // BZ
    same = (
        (layer_blocks[:-1] == layer_blocks[1:]).astype(jnp.float32).reshape(layers - 1, 1, 1),
        (map_x[:-1] == map_x[1:]).astype(jnp.float32).reshape(1, span_x - 1, 1),
        (map_y[:-1] == map_y[1:]).astype(jnp.float32).reshape(1, 1, span_y - 1),
    )
    couple = tuple(
        (
            trans[axis] * lower(extended_basis, axis) * upper(extended_basis, axis)
            for axis in range(3)
        )
    )
    inner = 0.0
    for axis in range(3):
        inner = inner + pad_after(couple[axis] * same[axis], axis)
    own_x = (
        map_x[:, None] == (index_x * blocks_x + jnp.arange(blocks_x, dtype=jnp.int32))[None, :]
    ).astype(jnp.float32)
    own_y = (
        map_y[:, None] == (index_y * blocks_y + jnp.arange(blocks_y, dtype=jnp.int32))[None, :]
    ).astype(jnp.float32)

    def to_blocks(field):
        summed = field.reshape(layers // BZ, BZ, span_x, span_y).sum(axis=1)
        partial_sum = jnp.einsum("zab,ak->zkb", summed, own_x, precision=highest)
        return jnp.einsum("zkb,bl->zkl", partial_sum, own_y, precision=highest)

    crossing = []
    for axis in range(3):
        cut = couple[axis] * (1.0 - same[axis])
        crossing.append(to_blocks(pad_after(cut, axis)))
        crossing.append(to_blocks(pad_before(cut, axis)))
    system = (to_blocks(extended_basis * residual), to_blocks(cell_diagonal - 2.0 * inner)) + tuple(
        crossing
    )
    estimate = relaxation * system[0] / system[1]
    for sweep in range(NSWEEP - 1):
        bordered = with_halo(estimate, (("gx", 1), ("gy", 2)), 1)
        estimate = relax(bordered, system)
    nearby = padded(estimate, (("gx", 1), ("gy", 2)), 1)
    near_x = (
        map_x[:, None]
        == (index_x * blocks_x - 1 + jnp.arange(blocks_x + 2, dtype=jnp.int32))[None, :]
    ).astype(jnp.float32)
    near_y = (
        map_y[:, None]
        == (index_y * blocks_y - 1 + jnp.arange(blocks_y + 2, dtype=jnp.int32))[None, :]
    ).astype(jnp.float32)
    fine_corr = jnp.einsum("zkl,ak->zal", nearby, near_x, precision=highest)
    fine_corr = jnp.einsum("zal,bl->zab", fine_corr, near_y, precision=highest)
    fine_corr = jnp.repeat(fine_corr, BZ, axis=0)
    new_press = extended_pressure + extended_basis * fine_corr
    flows = tuple(
        (trans[axis] * (lower(new_press, axis) - upper(new_press, axis)) for axis in range(3))
    )
    clamped_porosity = jnp.where(extended_porosity > 0, extended_porosity, 1.0)
    water_saturation = ext_water
    for substep in range(NSUB):
        water_saturation = march_forward(
            water_saturation,
            tuple((trim_border(member, substep) for member in flows)),
            trim_border(source, substep),
            trim_border(clamped_porosity, substep),
        )
    return (trim_border(new_press, border_width), water_saturation)


def solution(mesh):
    return jax.shard_map(
        body,
        mesh=mesh,
        in_specs=(
            P("member", "gx", "gy"),
            P("member", "gx", "gy"),
            P(),
            P(),
            P("member", "gx", "gy"),
            P("member", "gx", "gy"),
            P("member", "gx", "gy"),
            P("member"),
            P("member"),
            P("member"),
            P("member"),
        ),
        out_specs=(P("member", "gx", "gy"), P("member", "gx", "gy")),
        check_vma=False,
    )
```

profile of v0, /device:TPU:65, one launch (start us, length us, event | category | flops | bytes accessed | tf_op | source)
XLA Modules:
  0.0 181.2 jit_solution(7412913359134672901)
XLA Ops:
  0.7 1.5 fusion.169
  3.1 1.5 fusion.168
  4.5 3.8 %fusion.66 = (f32[160,8,128]{2,0,1:T(8,128)S(1)}, pred[32,8,128]{2,0,1:T(8,128)(4,1)S(1)}, pred[32,8,128]{2,0,1:T(8,128)(4,1)S(1)}, pred[32,8,128]{2,0,1:T(8,128)(4,1)S(1)}, pred[32,8,128]{2,0,1:T(8,128)(4,1)S(1)}) fusion(f32[160,8,128]{2,0,1:T(8,128)S(1)} %copy_dynamic-update-slice_fusion.1, f32[32,8,128]{2,1,0:T(8,128)} %param.11, ...), kind=kLoop, calls=%fused_computation.147 | loop fusion | flops 589824 | bytes 655376
  9.2 2.5 %add_dynamic-update-slice_fusion = f32[160,8,128]{2,0,1:T(8,128)S(1)} fusion(f32[160,8,128]{2,0,1:T(8,128)S(1)} %copy_dynamic-update-slice_fusion, pred[32,8,128]{2,0,1:T(8,128)(4,1)S(1)} %get-tuple-element.38, pred[32,8,128]{2,0,1:T(8,128)(4,1)S(1)} %get-tuple-element.37, pred[32,8,128]{2,0,1:T(8,128)(4,1)S(1)} %get-tuple-element.36, ...), kind=kLoop, calls=%fused_computation.151 | loop fusion | flops 229376 | bytes 262160
  12.7 4.6 %collective-permute-start = (f32[160,4,128]{2,0,1:T(8,128)S(1)}, f32[160,4,128]{2,0,1:T(8,128)S(1)}, u32[]{:S(2)}, u32[]{:S(2)}) collective-permute-start(f32[160,4,128]{2,0,1:T(8,128)S(1)} %get-tuple-element.51), channel_id=1, source_target_pairs={{0,16},{16,32},{32,48},{48,64},{64,80},{80,96},{96,112},{112,128},... | collective-permute-start | bytes 983048 | tf_op jit(solution)/shard_map/ppermute | solution.py:28
  17.3 40.1 %collective-permute-start.1 = (f32[160,4,128]{2,0,1:T(8,128)S(1)}, f32[160,4,128]{2,0,1:T(8,128)S(1)}, u32[]{:S(2)}, u32[]{:S(2)}) collective-permute-start(f32[160,4,128]{2,0,1:T(8,128)S(1)} %get-tuple-element.52), channel_id=1, source_target_pairs={{16,0},{32,16},{48,32},{64,48},{80,64},{96,80},{112,96},{128,112},... | collective-permute-start | bytes 983048 | tf_op jit(solution)/shard_map/ppermute | solution.py:31
  68.4 1.4 slice.496
  71.9 1.6 copy.88
  73.5 1.6 copy.89
  75.1 3.0 %pad_maximum_fusion = f32[160,16,136]{2,0,1:T(8,128)S(1)} fusion(f32[160,16,4]{2,0,1:T(8,128)} %copy.89, f32[160,4,128]{2,0,1:T(8,128)} %copy-done.8, f32[160,8,128]{2,0,1:T(8,128)S(1)} %copy_dynamic-update-slice_fusion.2, f32[160,4,128]{2,0,1:T(8,128)} %copy-done.7, f32[160,16,4]{2,0,1:T(8,128)} %copy.88), kind=kLoop, calls=%fused_computation | loop fusion | flops 1392640 | bytes 2785280 | tf_op jit(solution)/shard_map/concatenate | solution.py:32
  85.7 4.7 %fusion.158 = (f32[32,16,136]{2,0,1:T(8,128)}, f32[32,16,136]{2,0,1:T(8,128)S(1)}, f32[32,16,136]{2,0,1:T(8,128)}, f32[32,16,136]{2,0,1:T(8,128)}, f32[32,16,136]{2,0,1:T(8,128)}, /*index=5*/f32[32,16,136]{2,0,1:T(8,128)}) fusion(f32[160,16,136]{2,0,1:T(8,128)S(1)} %pad_maximum_fusion, f32[32,16,135]{2,0,1:T(8,128)} %get-tuple-element.42, ...), kind=kLoop, calls=%fused_computation.293 | loop fusion | flops 1462272 | bytes 4391424 | tf_op jit(solution)/shard_map/slice | solution.py:87
  90.5 2.0 %reshape.135 = f32[8,4,16,136]{3,1,0,2:T(4,128)} reshape(f32[32,16,136]{2,0,1:T(8,128)} %get-tuple-element.48) | data formatting | bytes 557056 | tf_op jit(solution)/shard_map/reshape | solution.py:236
  96.1 2.0 %collective-permute-start.4 = (f32[8,1,16]{2,0,1:T(8,128)S(1)}, f32[8,1,16]{2,0,1:T(8,128)S(1)}, u32[]{:S(2)}, u32[]{:S(2)}) collective-permute-start(f32[8,1,16]{2,0,1:T(8,128)S(1)} %get-tuple-element.71), channel_id=1, source_target_pairs={{16,0},{32,16},{48,32},{64,48},{80,64},{96,80},{112,96},{128,112},... | collective-permute-start | bytes 1544 | tf_op jit(solution)/shard_map/ppermute | solution.py:45
  98.1 3.7 %collective-permute-start.5 = (f32[8,1,16]{2,0,1:T(8,128)S(1)}, f32[8,1,16]{2,0,1:T(8,128)S(1)}, u32[]{:S(2)}, u32[]{:S(2)}) collective-permute-start(f32[8,1,16]{2,0,1:T(8,128)S(1)} %get-tuple-element.71), channel_id=1, source_target_pairs={{0,16},{16,32},{32,48},{48,64},{64,80},{80,96},{96,112},{112,128},... | collective-permute-start | bytes 1544 | tf_op jit(solution)/shard_map/ppermute | solution.py:44
  101.8 3.2 %fusion.162 = (f32[32,16,136]{2,0,1:T(8,128)}, f32[32,16,136]{2,0,1:T(8,128)}, f32[32,16,136]{2,0,1:T(8,128)}, f32[32,16,136]{2,0,1:T(8,128)}) fusion(f32[32,16,135]{2,0,1:T(8,128)} %get-tuple-element.28, f32[32,15,136]{2,0,1:T(8,128)} %get-tuple-element.24), kind=kLoop, calls=%fused_computation.297 | loop fusion | bytes 1651712 | tf_op jit(solution)/shard_map/jit(_pad)/pad | solution.py:66
  104.9 2.0 %reshape.139 = f32[8,4,16,136]{3,1,0,2:T(4,128)} reshape(f32[32,16,136]{2,0,1:T(8,128)} %get-tuple-element.95) | data formatting | bytes 557056 | tf_op jit(solution)/shard_map/reshape | solution.py:236
  108.7 2.0 %reshape.138 = f32[8,4,16,136]{3,1,0,2:T(4,128)} reshape(f32[32,16,136]{2,0,1:T(8,128)} %get-tuple-element.96) | data formatting | bytes 557056 | tf_op jit(solution)/shard_map/reshape | solution.py:236
  112.5 2.0 %reshape.141 = f32[8,4,16,136]{3,1,0,2:T(4,128)} reshape(f32[32,16,136]{2,0,1:T(8,128)} %get-tuple-element.57) | data formatting | bytes 557056 | tf_op jit(solution)/shard_map/reshape | solution.py:236
  116.1 2.0 %reshape.140 = f32[8,4,16,136]{3,1,0,2:T(4,128)} reshape(f32[32,16,136]{2,0,1:T(8,128)} %get-tuple-element.56) | data formatting | bytes 557056 | tf_op jit(solution)/shard_map/reshape | solution.py:236
  119.8 1.5 collective-permute-start.6
  121.4 4.7 %collective-permute-start.7 = (f32[8,1,1]{2,0,1:T(8,128)S(1)}, f32[8,1,1]{2,0,1:T(8,128)S(1)}, u32[]{:S(2)}, u32[]{:S(2)}) collective-permute-start(f32[8,1,1]{2,0,1:T(8,128)S(1)} %get-tuple-element.79), channel_id=1, source_target_pairs={{0,1},{1,2},{2,3},{3,4},{4,5},{5,6},{6,7},{7,8},{8,9},{9,10},{10,1... | collective-permute-start | bytes 104 | tf_op jit(solution)/shard_map/ppermute | solution.py:44
  126.0 2.0 %reshape.137 = f32[8,4,16,136]{3,1,0,2:T(4,128)} reshape(f32[32,16,136]{2,0,1:T(8,128)} %get-tuple-element.93) | data formatting | bytes 557056 | tf_op jit(solution)/shard_map/reshape | solution.py:236
  129.8 2.0 %reshape.136 = f32[8,4,16,136]{3,1,0,2:T(4,128)} reshape(f32[32,16,136]{2,0,1:T(8,128)} %get-tuple-element.94) | data formatting | bytes 557056 | tf_op jit(solution)/shard_map/reshape | solution.py:236
  134.0 2.0 %collective-permute-start.8 = (f32[8,1,16]{2,0,1:T(8,128)S(1)}, f32[8,1,16]{2,0,1:T(8,128)S(1)}, u32[]{:S(2)}, u32[]{:S(2)}) collective-permute-start(f32[8,1,16]{2,0,1:T(8,128)S(1)} %get-tuple-element.90), channel_id=1, source_target_pairs={{16,0},{32,16},{48,32},{64,48},{80,64},{96,80},{112,96},{128,112},... | collective-permute-start | bytes 1544 | tf_op jit(solution)/shard_map/ppermute | solution.py:45
  135.9 3.7 %collective-permute-start.9 = (f32[8,1,16]{2,0,1:T(8,128)S(1)}, f32[8,1,16]{2,0,1:T(8,128)S(1)}, u32[]{:S(2)}, u32[]{:S(2)}) collective-permute-start(f32[8,1,16]{2,0,1:T(8,128)S(1)} %get-tuple-element.90), channel_id=1, source_target_pairs={{0,16},{16,32},{32,48},{48,64},{64,80},{80,96},{96,112},{112,128},... | collective-permute-start | bytes 1544 | tf_op jit(solution)/shard_map/ppermute | solution.py:44
  140.9 4.0 %collective-permute-start.11 = (f32[8,1,1]{2,0,1:T(8,128)S(1)}, f32[8,1,1]{2,0,1:T(8,128)S(1)}, u32[]{:S(2)}, u32[]{:S(2)}) collective-permute-start(f32[8,1,1]{2,0,1:T(8,128)S(1)} %get-tuple-element.75), channel_id=1, source_target_pairs={{0,1},{1,2},{2,3},{3,4},{4,5},{5,6},{6,7},{7,8},{8,9},{9,10},{10,1... | collective-permute-start | bytes 104 | tf_op jit(solution)/shard_map/ppermute | solution.py:44
  145.8 3.1 %collective-permute-start.12 = (f32[8,1,16]{2,0,1:T(8,128)S(1)}, f32[8,1,16]{2,0,1:T(8,128)S(1)}, u32[]{:S(2)}, u32[]{:S(2)}) collective-permute-start(f32[8,1,16]{2,0,1:T(8,128)S(1)} %fusion.116), channel_id=1, source_target_pairs={{0,16},{16,32},{32,48},{48,64},{64,80},{80,96},{96,112},{112,128},... | collective-permute-start | bytes 1544 | tf_op jit(solution)/shard_map/ppermute | solution.py:28
  148.9 2.0 %collective-permute-start.13 = (f32[8,1,16]{2,0,1:T(8,128)S(1)}, f32[8,1,16]{2,0,1:T(8,128)S(1)}, u32[]{:S(2)}, u32[]{:S(2)}) collective-permute-start(f32[8,1,16]{2,0,1:T(8,128)S(1)} %fusion.116), channel_id=1, source_target_pairs={{16,0},{32,16},{48,32},{64,48},{80,64},{96,80},{112,96},{128,112},... | collective-permute-start | bytes 1544 | tf_op jit(solution)/shard_map/ppermute | solution.py:31
  154.0 1.8 %slice.535 = f32[32,10,130]{2,0,1:T(8,128)} slice(f32[32,16,136]{2,0,1:T(8,128)} %get-tuple-element.47), slice={[0:32], [3:13], [3:133]} | slice | bytes 332800 | tf_op jit(solution)/shard_map/slice | solution.py:77
  155.9 3.9 %collective-permute-start.14 = (f32[8,3,1]{2,0,1:T(8,128)S(1)}, f32[8,3,1]{2,0,1:T(8,128)S(1)}, u32[]{:S(2)}, u32[]{:S(2)}) collective-permute-start(f32[8,3,1]{2,0,1:T(8,128)S(1)} %get-tuple-element.68), channel_id=1, source_target_pairs={{0,1},{1,2},{2,3},{3,4},{4,5},{5,6},{6,7},{7,8},{8,9},{9,10},{10,1... | collective-permute-start | bytes 296 | tf_op jit(solution)/shard_map/ppermute | solution.py:28
  161.2 3.2 %collective-permute-done.15 = f32[8,3,1]{2,0,1:T(8,128)S(1)} collective-permute-done((f32[8,3,1]{2,0,1:T(8,128)S(1)}, f32[8,3,1]{2,0,1:T(8,128)S(1)}, u32[]{:S(2)}, u32[]{:S(2)}) %collective-permute-start.15) | collective-permute-done | bytes 128 | tf_op jit(solution)/shard_map/ppermute | solution.py:31
  167.2 2.0 %reshape.142 = f32[32,16,136]{2,0,1:T(8,128)} reshape(f32[8,4,16,136]{3,1,0,2:T(4,128)} %broadcast_in_dim.116) | data formatting | bytes 557056 | tf_op jit(solution)/shard_map/reshape | solution.py:263
  (177 shorter events, 59.0 us)
Async XLA Ops:
  0.6 57.3 %copy-start.22 = (s32[512]{0:T(512)S(1)}, s32[512]{0:T(512)}, u32[]{:S(2)}) copy-start(s32[512]{0:T(512)} %param.20) | copy-start | bytes 6148
  0.6 57.3 %copy-start.26 = (f32[512]{0:T(512)S(1)}, f32[512]{0:T(512)}, u32[]{:S(2)}) copy-start(f32[512]{0:T(512)} %param.21) | copy-start | bytes 6148
  0.7 58.7 %copy-start.17 = (s32[2048]{0:T(1024)S(1)}, s32[2048]{0:T(1024)}, u32[]{:S(2)}) copy-start(s32[2048]{0:T(1024)} %param.19) | copy-start | bytes 24580
  0.7 59.4 %copy-start.25 = (s32[128]{0:T(128)S(1)}, s32[128]{0:T(128)}, u32[]{:S(2)}) copy-start(s32[128]{0:T(128)} %param.18) | copy-start | bytes 1540
  12.7 49.3 %collective-permute-start = (f32[160,4,128]{2,0,1:T(8,128)S(1)}, f32[160,4,128]{2,0,1:T(8,128)S(1)}, u32[]{:S(2)}, u32[]{:S(2)}) collective-permute-start(f32[160,4,128]{2,0,1:T(8,128)S(1)} %get-tuple-element.51), channel_id=1, source_target_pairs={{0,16},{16,32},{32,48},{48,64},{64,80},{80,96},{96,112},{112,128},... | collective-permute-start | bytes 983048 | tf_op jit(solution)/shard_map/ppermute | solution.py:28
  17.3 44.7 %collective-permute-start.1 = (f32[160,4,128]{2,0,1:T(8,128)S(1)}, f32[160,4,128]{2,0,1:T(8,128)S(1)}, u32[]{:S(2)}, u32[]{:S(2)}) collective-permute-start(f32[160,4,128]{2,0,1:T(8,128)S(1)} %get-tuple-element.52), channel_id=1, source_target_pairs={{16,0},{32,16},{48,32},{64,48},{80,64},{96,80},{112,96},{128,112},... | collective-permute-start | bytes 983048 | tf_op jit(solution)/shard_map/ppermute | solution.py:31
  59.5 74.2 %copy-start.16 = (s32[136]{0:T(256)}, s32[136]{0:T(256)S(1)}, u32[]{:S(2)}) copy-start(s32[136]{0:T(256)S(1)} %pad_dynamic-slice_fusion) | copy-start | bytes 1636
  60.2 3.8 %copy-start.18 = (s32[16]{0:T(128)}, s32[16]{0:T(128)S(1)}, u32[]{:S(2)}) copy-start(s32[16]{0:T(128)S(1)} %get-tuple-element.33) | copy-start | bytes 196
  64.6 7.2 %collective-permute-start.2 = (f32[160,16,4]{0,1,2:T(8,128)S(1)}, f32[160,16,4]{0,1,2:T(8,128)S(1)}, u32[]{:S(2)}, u32[]{:S(2)}) collective-permute-start(f32[160,16,4]{0,1,2:T(8,128)S(1)} %copy.86), channel_id=1, source_target_pairs={{0,1},{1,2},{2,3},{3,4},{4,5},{5,6},{6,7},{7,8},{8,9},{9,10},{10,1... | collective-permute-start | bytes 122888 | tf_op jit(solution)/shard_map/ppermute | solution.py:28
  66.6 6.9 %collective-permute-start.3 = (f32[160,16,4]{0,1,2:T(8,128)S(1)}, f32[160,16,4]{0,1,2:T(8,128)S(1)}, u32[]{:S(2)}, u32[]{:S(2)}) collective-permute-start(f32[160,16,4]{0,1,2:T(8,128)S(1)} %copy.87), channel_id=1, source_target_pairs={{1,0},{2,1},{3,2},{4,3},{5,4},{6,5},{7,6},{8,7},{9,8},{10,9},{11,1... | collective-permute-start | bytes 122888 | tf_op jit(solution)/shard_map/ppermute | solution.py:31
  78.1 2.2 %copy-start.23 = (f32[31]{0:T(128)S(1)}, f32[31]{0:T(128)}, u32[]{:S(2)}) copy-start(f32[31]{0:T(128)} %get-tuple-element.22) | copy-start | bytes 376
  79.2 4.1 %copy-start = (f32[32,16,135]{2,0,1:T(8,128)}, f32[32,16,135]{2,0,1:T(8,128)S(1)}, u32[]{:S(2)}) copy-start(f32[32,16,135]{2,0,1:T(8,128)S(1)} %get-tuple-element.29) | copy-start | bytes 829444
  79.2 2.1 %copy-start.24 = (f32[31]{0:T(128)S(1)}, f32[31]{0:T(128)}, u32[]{:S(2)}) copy-start(f32[31]{0:T(128)} %get-tuple-element.23) | copy-start | bytes 376
  80.2 2.1 %copy-start.3 = (f32[32,15,136]{2,0,1:T(8,128)}, f32[32,15,136]{2,0,1:T(8,128)S(1)}, u32[]{:S(2)}) copy-start(f32[32,15,136]{2,0,1:T(8,128)S(1)} %get-tuple-element.25) | copy-start | bytes 783364
  81.3 2.0 %copy-start.2 = (f32[31,16,136]{2,0,1:T(8,128)}, f32[31,16,136]{2,0,1:T(8,128)S(1)}, u32[]{:S(2)}) copy-start(f32[31,16,136]{2,0,1:T(8,128)S(1)} %get-tuple-element.21) | copy-start | bytes 809476
  90.5 5.1 %copy-start.27 = (s32[16]{0:T(128)S(1)}, s32[16]{0:T(128)}, u32[]{:S(2)}) copy-start(s32[16]{0:T(128)} %iota_add_fusion.2) | copy-start | bytes 196
  96.1 37.5 %collective-permute-start.4 = (f32[8,1,16]{2,0,1:T(8,128)S(1)}, f32[8,1,16]{2,0,1:T(8,128)S(1)}, u32[]{:S(2)}, u32[]{:S(2)}) collective-permute-start(f32[8,1,16]{2,0,1:T(8,128)S(1)} %get-tuple-element.71), channel_id=1, source_target_pairs={{16,0},{32,16},{48,32},{64,48},{80,64},{96,80},{112,96},{128,112},... | collective-permute-start | bytes 1544 | tf_op jit(solution)/shard_map/ppermute | solution.py:45
  98.1 35.5 %collective-permute-start.5 = (f32[8,1,16]{2,0,1:T(8,128)S(1)}, f32[8,1,16]{2,0,1:T(8,128)S(1)}, u32[]{:S(2)}, u32[]{:S(2)}) collective-permute-start(f32[8,1,16]{2,0,1:T(8,128)S(1)} %get-tuple-element.71), channel_id=1, source_target_pairs={{0,16},{16,32},{32,48},{48,64},{64,80},{80,96},{96,112},{112,128},... | collective-permute-start | bytes 1544 | tf_op jit(solution)/shard_map/ppermute | solution.py:44
  112.5 17.1 %copy-start.28 = (s32[16]{0:T(128)S(1)}, s32[16]{0:T(128)}, u32[]{:S(2)}) copy-start(s32[16]{0:T(128)} %iota_add_fusion.2) | copy-start | bytes 196
  119.8 13.8 %collective-permute-start.6 = (f32[8,1,1]{2,0,1:T(8,128)S(1)}, f32[8,1,1]{2,0,1:T(8,128)S(1)}, u32[]{:S(2)}, u32[]{:S(2)}) collective-permute-start(f32[8,1,1]{2,0,1:T(8,128)S(1)} %get-tuple-element.78), channel_id=1, source_target_pairs={{1,0},{2,1},{3,2},{4,3},{5,4},{6,5},{7,6},{8,7},{9,8},{10,9},{11,1... | collective-permute-start | bytes 104 | tf_op jit(solution)/shard_map/ppermute | solution.py:45
  121.4 12.3 %collective-permute-start.7 = (f32[8,1,1]{2,0,1:T(8,128)S(1)}, f32[8,1,1]{2,0,1:T(8,128)S(1)}, u32[]{:S(2)}, u32[]{:S(2)}) collective-permute-start(f32[8,1,1]{2,0,1:T(8,128)S(1)} %get-tuple-element.79), channel_id=1, source_target_pairs={{0,1},{1,2},{2,3},{3,4},{4,5},{5,6},{6,7},{7,8},{8,9},{9,10},{10,1... | collective-permute-start | bytes 104 | tf_op jit(solution)/shard_map/ppermute | solution.py:44
  134.0 11.8 %collective-permute-start.8 = (f32[8,1,16]{2,0,1:T(8,128)S(1)}, f32[8,1,16]{2,0,1:T(8,128)S(1)}, u32[]{:S(2)}, u32[]{:S(2)}) collective-permute-start(f32[8,1,16]{2,0,1:T(8,128)S(1)} %get-tuple-element.90), channel_id=1, source_target_pairs={{16,0},{32,16},{48,32},{64,48},{80,64},{96,80},{112,96},{128,112},... | collective-permute-start | bytes 1544 | tf_op jit(solution)/shard_map/ppermute | solution.py:45
  135.9 9.8 %collective-permute-start.9 = (f32[8,1,16]{2,0,1:T(8,128)S(1)}, f32[8,1,16]{2,0,1:T(8,128)S(1)}, u32[]{:S(2)}, u32[]{:S(2)}) collective-permute-start(f32[8,1,16]{2,0,1:T(8,128)S(1)} %get-tuple-element.90), channel_id=1, source_target_pairs={{0,16},{16,32},{32,48},{48,64},{64,80},{80,96},{96,112},{112,128},... | collective-permute-start | bytes 1544 | tf_op jit(solution)/shard_map/ppermute | solution.py:44
  139.6 5.4 %collective-permute-start.10 = (f32[8,1,1]{2,0,1:T(8,128)S(1)}, f32[8,1,1]{2,0,1:T(8,128)S(1)}, u32[]{:S(2)}, u32[]{:S(2)}) collective-permute-start(f32[8,1,1]{2,0,1:T(8,128)S(1)} %get-tuple-element.74), channel_id=1, source_target_pairs={{1,0},{2,1},{3,2},{4,3},{5,4},{6,5},{7,6},{8,7},{9,8},{10,9},{11,1... | collective-permute-start | bytes 104 | tf_op jit(solution)/shard_map/ppermute | solution.py:45
  140.9 4.8 %collective-permute-start.11 = (f32[8,1,1]{2,0,1:T(8,128)S(1)}, f32[8,1,1]{2,0,1:T(8,128)S(1)}, u32[]{:S(2)}, u32[]{:S(2)}) collective-permute-start(f32[8,1,1]{2,0,1:T(8,128)S(1)} %get-tuple-element.75), channel_id=1, source_target_pairs={{0,1},{1,2},{2,3},{3,4},{4,5},{5,6},{6,7},{7,8},{8,9},{9,10},{10,1... | collective-permute-start | bytes 104 | tf_op jit(solution)/shard_map/ppermute | solution.py:44
  145.8 10.0 %collective-permute-start.12 = (f32[8,1,16]{2,0,1:T(8,128)S(1)}, f32[8,1,16]{2,0,1:T(8,128)S(1)}, u32[]{:S(2)}, u32[]{:S(2)}) collective-permute-start(f32[8,1,16]{2,0,1:T(8,128)S(1)} %fusion.116), channel_id=1, source_target_pairs={{0,16},{16,32},{32,48},{48,64},{64,80},{80,96},{96,112},{112,128},... | collective-permute-start | bytes 1544 | tf_op jit(solution)/shard_map/ppermute | solution.py:28
  148.9 7.0 %collective-permute-start.13 = (f32[8,1,16]{2,0,1:T(8,128)S(1)}, f32[8,1,16]{2,0,1:T(8,128)S(1)}, u32[]{:S(2)}, u32[]{:S(2)}) collective-permute-start(f32[8,1,16]{2,0,1:T(8,128)S(1)} %fusion.116), channel_id=1, source_target_pairs={{16,0},{32,16},{48,32},{64,48},{80,64},{96,80},{112,96},{128,112},... | collective-permute-start | bytes 1544 | tf_op jit(solution)/shard_map/ppermute | solution.py:31
  155.9 5.3 %collective-permute-start.14 = (f32[8,3,1]{2,0,1:T(8,128)S(1)}, f32[8,3,1]{2,0,1:T(8,128)S(1)}, u32[]{:S(2)}, u32[]{:S(2)}) collective-permute-start(f32[8,3,1]{2,0,1:T(8,128)S(1)} %get-tuple-element.68), channel_id=1, source_target_pairs={{0,1},{1,2},{2,3},{3,4},{4,5},{5,6},{6,7},{7,8},{8,9},{9,10},{10,1... | collective-permute-start | bytes 296 | tf_op jit(solution)/shard_map/ppermute | solution.py:28
  159.8 4.5 %collective-permute-start.15 = (f32[8,3,1]{2,0,1:T(8,128)S(1)}, f32[8,3,1]{2,0,1:T(8,128)S(1)}, u32[]{:S(2)}, u32[]{:S(2)}) collective-permute-start(f32[8,3,1]{2,0,1:T(8,128)S(1)} %get-tuple-element.69), channel_id=1, source_target_pairs={{1,0},{2,1},{3,2},{4,3},{5,4},{6,5},{7,6},{8,7},{9,8},{10,9},{11,1... | collective-permute-start | bytes 296 | tf_op jit(solution)/shard_map/ppermute | solution.py:31
  169.3 2.4 %copy-start.4 = (f32[32,15,136]{2,0,1:T(8,128)S(1)}, f32[32,15,136]{2,0,1:T(8,128)}, u32[]{:S(2)}) copy-start(f32[32,15,136]{2,0,1:T(8,128)} %copy-done.3) | copy-start | bytes 783364
  172.7 1.2 copy-start.11
  172.7 1.2 copy-start.12
  (13 other events, 11.6 us)
where the time goes:
time: 184 us; the launch traced here: 181 us
  starting transfers between devices  80.3 us (44%)
  local copies, waits for them, and re-layouts  45.4 us (25%)
  other arithmetic  43.8 us (24%)
  matrix products  6.35 us (3%)
  waiting for transfers between devices  3.93 us (2%)
    ppermute x4, starting transfers between devices, padded(): lax.ppermute(lax.slice_in_dim(block, 0, width, axis=dim), axis, backward)  44.7 us
    ppermute x4, starting transfers between devices, with_halo(): lax.ppermute(last, axis, up)  16.1 us
    reshape x8, local copies, waits for them, and re-layouts, to_blocks(): summed = field.reshape(layers // BZ, BZ, span_x, span_y).sum(axis=1)  15 us
    ppermute x4, starting transfers between devices, padded(): lax.ppermute(lax.slice_in_dim(block, block.shape[dim] - width, None, axis...  12.9 us
    reduce_sum x8, other arithmetic, to_blocks(): summed = field.reshape(layers // BZ, BZ, span_x, span_y).sum(axis=1)  10.9 us
    slice x11, local copies, waits for them, and re-layouts, trim_border(): field[:, border_width:field.shape[1] - border_width, border_width:field.s...  8.55 us
    ppermute x4, starting transfers between devices, with_halo(): lax.ppermute(first, axis, [(b, a) for a, b in up])  6.72 us
    unnamed x62, local copies, waits for them, and re-layouts  6.62 us
  transfers between devices with their start and end apart: 16, of which 2 were waited for; matrix products, arithmetic and copies ran while one was open for 23% of the time, Pallas kernels for 0%

commit v1 on v0

v1 whole, which is shorter than its diff:
```python
import jax
import jax.numpy as jnp
from jax import lax
from jax.experimental import pallas as pl
from jax.experimental.pallas import tpu as pltpu
from jax.sharding import PartitionSpec as P

NZ = 32
BX = 8
BY = 8
BZ = 4
NSWEEP = 3
NSUB = 4
NFAC = 4
NXL = 8
NYL = 128
EXT = NYL + 8
GROUPS = 4
ROWS_C = 24
REACH = 4

time_step = 0.005
MESH = pl.DeviceIdType.MESH
f32 = jnp.float32
bf16 = jnp.bfloat16
M, PR, B, S, PHI = range(5)


def iota(shape, dim):
    return lax.broadcasted_iota(jnp.int32, shape, dim)


def harmonic(left, right):
    total = left + right
    return 2.0 * left * right / jnp.where(total > 0, total, 1.0)


def split2(v):
    hi = v.astype(bf16)
    return hi, (v - hi.astype(f32)).astype(bf16)


def split3(v):
    hi = v.astype(bf16)
    rest = v - hi.astype(f32)
    mid = rest.astype(bf16)
    return hi, mid, (rest - mid.astype(f32)).astype(bf16)


def nn(a, b):
    return lax.dot_general(a, b, (((1,), (0,)), ((), ())), preferred_element_type=f32)


def nt(a, b):
    return lax.dot_general(a, b, (((1,), (1,)), ((), ())), preferred_element_type=f32)


def roll(v, shift, axis):
    return pltpu.roll(v, shift % v.shape[axis], axis)


def next_x(here, after):
    lane = iota(here.shape, 1)
    return jnp.where(lane < 96, roll(here, -32, 1), roll(after, -32, 1))


def prev_x(here, before):
    lane = iota(here.shape, 1)
    return jnp.where(lane >= 32, roll(here, 32, 1), roll(before, 32, 1))


def comm_kernel(
    sizes,
    perm, fac, pres, sat, bas, bymap, wells, rates, bxmap, fpor, fmob,
    fx_out, fy_out, fz_out, s_out, w_out, src_out, np_out,
    mob, por, newp, E, yh, xs, xr, ys, yr, ps, low, high,
    send_a, recv_a, send_h, recv_h, send_c, recv_c,
):
    n_gx, n_gy, full_y = sizes
    gx = lax.axis_index("gx")
    gy = lax.axis_index("gy")

    def there(dx, dy):
        ok = jnp.bool_(True)
        if dx:
            ok = ok & (gx + dx >= 0) & (gx + dx < n_gx)
        if dy:
            ok = ok & (gy + dy >= 0) & (gy + dy < n_gy)
        return ok

    def where_is(dx, dy):
        return {"gx": gx + dx, "gy": gy + dy}

    partners = [(dx, dy) for dx in range(-REACH, REACH + 1) for dy in (-1, 0, 1) if (dx, dy) != (0, 0)]

    at_edge = (gx < REACH) | (gx >= n_gx - REACH) | (gy == 0) | (gy == n_gy - 1)

    @pl.when(at_edge)
    def _():
        xr[...] = jnp.zeros_like(xr)
        yr[...] = jnp.zeros_like(yr)
        yh[...] = jnp.zeros_like(yh)
        ps[...] = jnp.zeros_like(ps)
        low[...] = jnp.zeros_like(low)
        high[...] = jnp.zeros_like(high)
        for f in range(5):
            E[f, 0] = jnp.zeros((EXT, 128), f32)
            E[f, 3] = jnp.zeros((EXT, 128), f32)

    barrier = pltpu.get_barrier_semaphore()
    for dx, dy in partners:
        @pl.when(there(dx, dy))
        def _(dx=dx, dy=dy):
            pl.semaphore_signal(barrier, inc=1, device_id=where_is(dx, dy), device_id_type=MESH)

    region = fac[...]
    s_nat = sat[...]
    fm = jnp.zeros(region.shape, f32)
    fp = jnp.zeros(region.shape, f32)
    for level in range(NFAC):
        fm = jnp.where(region == level, fmob[level], fm)
        fp = jnp.where(region == level, fpor[level], fp)
    mob[...] = perm[...] * fm * (s_nat * s_nat + (1.0 - s_nat) * (1.0 - s_nat) * 0.25)
    por[...] = fp

    def column(ref, x):
        return ref[pl.ds(x, NZ, NXL), :]

    own_edge = []
    for side, x in ((0, 0), (1, NXL - 1)):
        edge = [column(mob, x), column(pres, x), column(bas, x)]
        own_edge.append(edge)
        for k in range(3):
            xs[side, NZ * k : NZ * (k + 1), :] = edge[k]

    for f, ref in ((M, mob), (PR, pres), (B, bas), (S, sat), (PHI, por)):
        for g in (1, 2):
            block = jnp.concatenate([column(ref, 4 * (g - 1) + i) for i in range(4)], axis=0)
            E[f, g, 0:NYL, :] = block.T

    ys[...] = jnp.zeros_like(ys)
    for side, y in ((0, 0), (1, NYL - 1)):
        for k, f in enumerate((M, PR, B)):
            for g in (1, 2):
                ys[side, 2 * k + g - 1 : 2 * k + g, :] = E[f, g, y : y + 1, :]

    span_x = lax.min(gx, REACH) + lax.min(n_gx - 1 - gx, REACH) + 1
    span_y = lax.min(gy, 1) + lax.min(n_gy - 1 - gy, 1) + 1
    pl.semaphore_wait(barrier, span_x * span_y - 1)

    class Copy:
        def __init__(self, src, dst, sends, recvs, slot_out, slot_in, dx, dy):
            self.dx, self.dy = dx, dy
            self.copy = pltpu.make_async_remote_copy(
                src_ref=src, dst_ref=dst, send_sem=sends.at[slot_out], recv_sem=recvs.at[slot_in],
                device_id=where_is(dx, dy), device_id_type=MESH,
            )

        def start(self):
            pl.when(there(self.dx, self.dy))(lambda: self.copy.start())

        def wait_send(self):
            pl.when(there(self.dx, self.dy))(lambda: self.copy.wait_send())

        def wait_recv(self):
            pl.when(there(-self.dx, -self.dy))(lambda: self.copy.wait_recv())

    edges = [
        Copy(xs.at[1], xr.at[0], send_a, recv_a, 0, 0, 1, 0),
        Copy(xs.at[0], xr.at[1], send_a, recv_a, 1, 1, -1, 0),
        Copy(ys.at[1], yr.at[0], send_a, recv_a, 2, 2, 0, 1),
        Copy(ys.at[0], yr.at[1], send_a, recv_a, 3, 3, 0, -1),
    ]
    for copy in edges:
        copy.start()

    def halo_x(k, fields):
        return [
            Copy(E.at[fields, 2, 0:NYL], E.at[fields, 0, 0:NYL], send_h, recv_h, 2 * k, 2 * k, 1, 0),
            Copy(E.at[fields, 1, 0:NYL], E.at[fields, 3, 0:NYL], send_h, recv_h, 2 * k + 1, 2 * k + 1, -1, 0),
        ]

    up, down = slice(NYL - 8, NYL), slice(0, 8)
    everything = slice(0, 5)
    halo_early = halo_x(0, slice(0, 3))
    halo_late = halo_x(1, slice(3, 5))
    halo_y = [
        Copy(E.at[everything, 1:3, up], yh.at[0, everything, 1:3], send_h, recv_h, 4, 4, 0, 1),
        Copy(E.at[everything, 1:3, down], yh.at[1, everything, 1:3], send_h, recv_h, 5, 5, 0, -1),
        Copy(E.at[everything, 2, up], yh.at[0, everything, 0], send_h, recv_h, 6, 6, 1, 1),
        Copy(E.at[everything, 1, up], yh.at[0, everything, 3], send_h, recv_h, 7, 7, -1, 1),
        Copy(E.at[everything, 2, down], yh.at[1, everything, 0], send_h, recv_h, 8, 8, 1, -1),
        Copy(E.at[everything, 1, down], yh.at[1, everything, 3], send_h, recv_h, 9, 9, -1, -1),
    ]
    for copy in halo_early + halo_y:
        copy.start()

    well_y = wells[...] % full_y
    well_x = wells[...] // full_y
    n_wells = wells.shape[1]
    row = iota((EXT, 1), 0)
    y_here = gy * NYL + jnp.where(row < NYL + 4, row, row - EXT)
    hits_y = (y_here == well_y).astype(f32).astype(bf16)
    x_here = gx * NXL - 4 + iota((16, 1), 0)
    hits_x = jnp.where(x_here == well_x, rates[...], 0.0)
    col = nt(hits_y, jnp.concatenate(split3(hits_x), axis=0))
    col = (col[:, 0:16] + col[:, 16:32] + col[:, 32:48]) * (1.0 / NZ)
    lane = iota((16, 512), 1)
    spread = (lane // NZ == iota((16, 512), 0)).astype(f32).astype(bf16)
    src = nn(jnp.concatenate(split3(col), axis=1), jnp.concatenate([spread] * 3, axis=0))
    for g in range(GROUPS):
        src_out[g] = src[:, 128 * g : 128 * (g + 1)]

    blocks_y = NYL // BY
    map_own = bymap[pl.ds(gy, 1), :] - (gy * blocks_y - 4)
    map_up = bymap[pl.ds(lax.min(gy + 1, n_gy - 1), 1), :] - (gy * blocks_y - 4)
    map_down = bymap[pl.ds(lax.max(gy - 1, 0), 1), :] - (gy * blocks_y - 4)
    sum_y = (iota((ROWS_C, NYL), 0) == map_own).astype(f32).astype(bf16)
    sum_y = jnp.concatenate([sum_y, sum_y], axis=1)

    def column_of(values):
        return jnp.broadcast_to(values.astype(f32), (128, 128)).T

    by_row = column_of(map_own)
    by_up = column_of(map_up)[0:8]
    by_down = column_of(map_down)[120:128]
    by_ext = jnp.concatenate([by_row, jnp.where(iota((8, 128), 0) < 4, by_up, by_down)], axis=0)
    spread_y = (by_ext[:, 0:ROWS_C] == iota((EXT, ROWS_C), 1).astype(f32)).astype(f32).astype(bf16)
    same_y = (by_row == jnp.concatenate([by_row[1:], by_row[:1]], axis=0)).astype(f32)

    kx = [bxmap[lax.clamp(0, gx * NXL - 4 + i, n_gx * NXL - 1)] - gx for i in range(16)]

    def lanes_of(values, shape):
        which = iota(shape, 1) // NZ
        total = jnp.zeros(shape, jnp.int32)
        for i, value in enumerate(values):
            total = jnp.where(which == i, value, total)
        return total

    z_block = (iota((1, 256), 1) % NZ) // BZ
    target = (lanes_of(kx[4:12], (1, 256)) + 1) * 8 + z_block
    sum_xz = (iota((128, 256), 0) == target).astype(f32).astype(bf16)
    sum_xz = jnp.concatenate([sum_xz, sum_xz], axis=1)

    lane128 = iota((NYL, 128), 1)
    row128 = iota((NYL, 128), 0)
    z_of = lane128 % NZ
    m = [E[M, g, 0:NYL, :] for g in (1, 2)]
    p = [E[PR, g, 0:NYL, :] for g in (1, 2)]
    b = [E[B, g, 0:NYL, :] for g in (1, 2)]
    phi = [E[PHI, g, 0:NYL, :] for g in (1, 2)]
    own_src = [src[0:NYL, 128 * g : 128 * (g + 1)] for g in (1, 2)]
    same_x = [lanes_of([(kx[4 + 4 * g + i] == kx[5 + 4 * g + i]).astype(jnp.int32) for i in range(4)], (1, 128)) for g in (0, 1)]

    def nx_(v, g):
        return next_x(v[0], v[1]) if g == 0 else roll(v[1], -32, 1)

    def ny_(v):
        return roll(v, -1, 0)

    def nz_(v):
        return roll(v, -1, 1)

    tx = [harmonic(m[0], nx_(m, 0)), jnp.where(lane128 < 96, harmonic(m[1], nx_(m, 1)), 0.0)]
    ty = [jnp.where(row128 < NYL - 1, harmonic(v, ny_(v)), 0.0) for v in m]
    tz = [jnp.where(z_of < NZ - 1, 0.1 * harmonic(v, nz_(v)), 0.0) for v in m]
    qx = [tx[g] * (p[g] - nx_(p, g)) for g in (0, 1)]
    sums = []
    for g in (0, 1):
        qy = ty[g] * (p[g] - ny_(p[g]))
        qz = tz[g] * (p[g] - nz_(p[g]))
        in_x = prev_x(qx[g], qx[0]) if g == 1 else jnp.where(lane128 >= 32, roll(qx[0], 32, 1), 0.0)
        t_in_x = prev_x(tx[g], tx[0]) if g == 1 else jnp.where(lane128 >= 32, roll(tx[0], 32, 1), 0.0)
        out = qx[g] - in_x + qy - roll(qy, 1, 0) + qz - roll(qz, 1, 1)
        resid = b[g] * (own_src[g] - out)
        cond = tx[g] + t_in_x + ty[g] + roll(ty[g], 1, 0) + tz[g] + roll(tz[g], 1, 1)
        cx = tx[g] * b[g] * nx_(b, g)
        cy = ty[g] * b[g] * ny_(b[g])
        cz = tz[g] * b[g] * nz_(b[g])
        keep_x = same_x[g].astype(f32)
        keep_z = (z_of % BZ != BZ - 1).astype(f32)
        diag = b[g] * b[g] * (0.5 * phi[g] + cond) - 2.0 * (cx * keep_x + cy * same_y + cz * keep_z)
        sums.append((resid, diag, cz * (1.0 - keep_z), cx * (1.0 - keep_x), cy * (1.0 - same_y)))
    inner = []
    for q in range(5):
        hi, mid = split2(jnp.concatenate([sums[0][q], sums[1][q]], axis=1))
        inner.append(nn(sum_y, jnp.concatenate([hi, mid], axis=0)))

    kinds = 5
    z_row = iota((1, kinds * NZ), 1)
    kind = z_row // NZ
    k_low, k_high, k_next = kx[4], kx[11], kx[12]
    together = k_high == k_next
    q_of = lanes_of([0, 1, jnp.where(together, 1, 3), 0, 1], (1, kinds * NZ))
    k_of = lanes_of([k_high, k_high, k_high, k_low, k_low], (1, kinds * NZ))
    scale = jnp.where((kind == 2) & together, -2.0, 1.0)
    lane_to = q_of * 24 + (k_of + 1) * 8 + (z_row % NZ) // BZ
    sum_edge = jnp.where(iota((128, kinds * NZ), 0) == lane_to, scale, 0.0).astype(bf16)
    sum_edge = jnp.concatenate([sum_edge, sum_edge], axis=1)

    for copy in edges:
        copy.wait_recv()

    fields = []
    m0, p0, b0 = [xr[0, NZ * k : NZ * (k + 1), :] for k in range(3)]
    m1, p1, b1 = [xr[1, NZ * k : NZ * (k + 1), :] for k in range(3)]
    (om0, op0, ob0), (om1, op1, ob1) = own_edge
    t1 = harmonic(om1, m1)
    t0 = harmonic(om0, m0)
    fields = [
        -ob1 * t1 * (op1 - p1), ob1 * ob1 * t1, ob1 * b1 * t1,
        -ob0 * t0 * (op0 - p0), ob0 * ob0 * t0,
    ]
    hi, mid = split2(jnp.concatenate(fields, axis=0))
    edge_x = nt(sum_y, jnp.concatenate([hi, mid], axis=1))
    hi, mid = split2(edge_x)
    edge_x = nt(jnp.concatenate([hi, mid], axis=1), sum_edge)

    def wide(ref, side, k):
        return jnp.concatenate([ref[side, 2 * k : 2 * k + 1, :], ref[side, 2 * k + 1 : 2 * k + 2, :]], axis=1)

    um, up_, ub = [wide(yr, 1, k) for k in range(3)]
    dm, dp, db = [wide(yr, 0, k) for k in range(3)]
    om1, op1, ob1 = [wide(ys, 1, k) for k in range(3)]
    om0, op0, ob0 = [wide(ys, 0, k) for k in range(3)]
    t1 = harmonic(om1, um)
    t0 = harmonic(om0, dm)
    rows = iota((ROWS_C, 1), 0)
    r_high = by_row[NYL - 1 : NYL, 0:1].astype(jnp.int32)
    r_low = by_row[0:1, 0:1].astype(jnp.int32)
    r_next = by_up[0:1, 0:1].astype(jnp.int32)
    at_high = rows == r_high
    at_low = rows == r_low
    same = r_high == r_next
    couple = ob1 * ub * t1
    zero = jnp.zeros_like(couple)
    inner[0] = inner[0] + jnp.where(at_high, -ob1 * t1 * (op1 - up_), 0.0) + jnp.where(at_low, -ob0 * t0 * (op0 - dp), 0.0)
    inner[1] = (
        inner[1] + jnp.where(at_high, ob1 * ob1 * t1 - 2.0 * jnp.where(same, couple, zero), 0.0)
        + jnp.where(at_low, ob0 * ob0 * t0, 0.0)
    )
    inner[4] = inner[4] + jnp.where(at_high, jnp.where(same, zero, couple), 0.0)
    hi, mid = split2(jnp.concatenate(inner, axis=0))
    partial = nt(jnp.concatenate([hi, mid], axis=1), sum_xz)
    mine = edge_x
    for q in range(5):
        mine = mine + roll(partial[ROWS_C * q : ROWS_C * (q + 1)], 24 * q, 1)
    ps[REACH] = mine

    def slot(dx):
        return REACH + dx

    coarse = []
    for dx in (4, -4, 3, -3, 2, -2, 1, -1, 0):
        if dx:
            coarse.append(Copy(ps.at[slot(0)], ps.at[slot(-dx)], send_c, recv_c, slot(dx), slot(-dx), dx, 0))
        coarse.append(
            Copy(ps.at[slot(0), 16:24], low.at[slot(-dx)], send_c, recv_c, 9 + slot(dx), 9 + slot(-dx), dx, 1)
        )
        coarse.append(
            Copy(ps.at[slot(0), 0:8], high.at[slot(-dx)], send_c, recv_c, 18 + slot(dx), 18 + slot(-dx), dx, -1)
        )
    for copy in coarse:
        copy.start()
    for copy in halo_late:
        copy.start()

    target = (lanes_of(kx, (1, 512)) + 3) * 8 + (iota((1, 512), 1) % NZ) // BZ
    spread_xz = (iota((64, 512), 0) == target).astype(f32).astype(bf16)
    spread_xz = jnp.concatenate([spread_xz] * 3, axis=0)

    for copy in halo_early + halo_y + halo_late:
        copy.wait_recv()
    take_up = iota((8, 128), 0) < 4
    for f in range(5):
        for g in range(GROUPS):
            E[f, g, NYL:EXT, :] = jnp.where(take_up, yh[1, f, g], yh[0, f, g])

    z_ext = iota((EXT, 128), 1) % NZ
    for g in range(GROUPS):
        after = min(g + 1, GROUPS - 1)
        here = E[M, g]
        fx_out[g] = harmonic(here, next_x(here, E[M, after]))
        fy_out[g] = harmonic(here, roll(here, -1, 0))
        fz_out[g] = jnp.where(z_ext < NZ - 1, 0.1 * harmonic(here, roll(here, -1, 1)), 0.0)
        s_out[g] = E[S, g]
        phi_here = E[PHI, g]
        w_out[g] = time_step / jnp.where(phi_here > 0, phi_here, 1.0)

    for copy in coarse:
        copy.wait_recv()

    lane24 = iota((ROWS_C, 128), 1)
    system = [jnp.zeros((ROWS_C, 128), f32) for _ in range(5)]
    for dx in range(-REACH, REACH + 1):
        k = slot(dx)
        part = jnp.concatenate([ps[k, 0:8] + low[k], ps[k, 8:16], ps[k, 16:24] + high[k]], axis=0)
        first = (dx + 2) * 8
        take = (lane24 >= max(first, 0)) & (lane24 < min(first + 24, 56))
        for q in range(5):
            system[q] = system[q] + jnp.where(take, roll(part, first - 24 * q, 1), 0.0)
    resid, diag, cz, cx, cy = system
    diag = jnp.where(diag > 0, diag, 1.0)
    half = 0.5 / diag
    fixed = half * resid
    estimate = fixed
    for _ in range(NSWEEP - 1):
        flow = (
            cz * roll(estimate, -1, 1) + roll(cz * estimate, 1, 1)
            + cx * roll(estimate, -8, 1) + roll(cx * estimate, 8, 1)
            + cy * roll(estimate, -1, 0) + roll(cy * estimate, 1, 0)
        )
        estimate = 0.5 * estimate + fixed + half * flow
    row24 = iota((ROWS_C, 128), 0)
    wanted = (row24 >= 3) & (row24 < 21) & (lane24 >= 16) & (lane24 < 40)
    estimate = jnp.where(wanted, estimate, 0.0)[:, 0:64]
    spread1 = nn(jnp.concatenate(split3(estimate), axis=1), spread_xz)
    fine = nn(jnp.concatenate([spread_y] * 3, axis=1), jnp.concatenate(split3(spread1), axis=0))

    for g in range(GROUPS):
        newp[g] = E[PR, g] + E[B, g] * fine[:, 128 * g : 128 * (g + 1)]
    for g in range(GROUPS):
        after = min(g + 1, GROUPS - 1)
        here = newp[g]
        fx_out[g] = fx_out[g] * (here - next_x(here, newp[after]))
        fy_out[g] = fy_out[g] * (here - roll(here, -1, 0))
        fz_out[g] = fz_out[g] * (here - roll(here, -1, 1))
        if g in (1, 2):
            np_out[g - 1] = here[0:NYL]

    for copy in edges + halo_early + halo_late + halo_y + coarse:
        copy.wait_send()


def transport_kernel(fx, fy, fz, s_in, w, src, np_in, np_out, s_out, s, out_x):
    for g in range(GROUPS):
        s[g] = s_in[g]
    for step in range(NSUB):
        last = step == NSUB - 1
        frac = []
        for g in range(GROUPS):
            v = s[g]
            wet = v * v
            frac.append(wet / (wet + (1.0 - v) * (1.0 - v) * 0.25))
        carried = []
        for g in range(GROUPS):
            flow = fx[g]
            after = frac[min(g + 1, GROUPS - 1)]
            carried.append(jnp.where(flow > 0, frac[g], next_x(frac[g], after)) * flow)
        for g in range(GROUPS):
            if last and g in (0, 3):
                continue
            flow = fy[g]
            cy = jnp.where(flow > 0, frac[g], roll(frac[g], -1, 0)) * flow
            flow = fz[g]
            cz = jnp.where(flow > 0, frac[g], roll(frac[g], -1, 1)) * flow
            cx = carried[g]
            out = cx - prev_x(cx, carried[max(g - 1, 0)]) + cy - roll(cy, 1, 0) + cz - roll(cz, 1, 1)
            source = src[g]
            change = jnp.maximum(source, 0.0) + jnp.minimum(source, 0.0) * frac[g] - out
            s[g] = s[g] + w[g] * change
    for g in (1, 2):
        for block, dst in ((s[g, 0:NYL, :], s_out), (np_in[g - 1], np_out)):
            back = block.T
            for i in range(4):
                dst[pl.ds(4 * (g - 1) + i, NZ, NXL), :] = back[NZ * i : NZ * (i + 1)]


def solution(mesh):
    n_gx, n_gy = mesh.shape["gx"], mesh.shape["gy"]
    vmem = pl.BlockSpec(memory_space=pltpu.VMEM)
    smem = pl.BlockSpec(memory_space=pltpu.SMEM)

    def body(perm, facies, fpor, fmob, pressure, saturation, basis, bx_map, by_map, well_cells, well_rates):
        assert pressure.shape == (NZ, NXL, NYL)
        flat = lambda a: a.reshape(NZ * NXL, NYL)
        sizes = (n_gx, n_gy, by_map.shape[0])
        wide = jax.ShapeDtypeStruct((GROUPS, EXT, 128), f32)
        own = jax.ShapeDtypeStruct((2, NYL, 128), f32)
        results = pl.pallas_call(
            lambda *refs: comm_kernel(sizes, *refs),
            name="exchange",
            out_shape=[wide] * 6 + [own],
            in_specs=[vmem] * 8 + [smem] * 3,
            out_specs=[vmem] * 7,
            scratch_shapes=[
                pltpu.VMEM((NZ * NXL, NYL), f32),
                pltpu.VMEM((NZ * NXL, NYL), f32),
                pltpu.VMEM((GROUPS, EXT, 128), f32),
                pltpu.VMEM((5, GROUPS, EXT, 128), f32),
                pltpu.VMEM((2, 5, GROUPS, 8, 128), f32),
                pltpu.VMEM((2, 3 * NZ, NYL), f32),
                pltpu.VMEM((2, 3 * NZ, NYL), f32),
                pltpu.VMEM((2, 8, 128), f32),
                pltpu.VMEM((2, 8, 128), f32),
                pltpu.VMEM((2 * REACH + 1, ROWS_C, 128), f32),
                pltpu.VMEM((2 * REACH + 1, 8, 128), f32),
                pltpu.VMEM((2 * REACH + 1, 8, 128), f32),
                pltpu.SemaphoreType.DMA((4,)),
                pltpu.SemaphoreType.DMA((4,)),
                pltpu.SemaphoreType.DMA((10,)),
                pltpu.SemaphoreType.DMA((10,)),
                pltpu.SemaphoreType.DMA((27,)),
                pltpu.SemaphoreType.DMA((27,)),
            ],
            compiler_params=pltpu.CompilerParams(collective_id=0, has_side_effects=True),
        )(
            flat(perm), flat(facies), flat(pressure), flat(saturation), flat(basis),
            by_map.reshape(n_gy, NYL), well_cells.reshape(1, -1), well_rates.reshape(1, -1),
            bx_map, fpor, fmob,
        )
        shape = jax.ShapeDtypeStruct((NZ * NXL, NYL), f32)
        new_pressure, water = pl.pallas_call(
            transport_kernel,
            name="transport",
            out_shape=[shape, shape],
            in_specs=[vmem] * 7,
            out_specs=[vmem] * 2,
            scratch_shapes=[pltpu.VMEM((GROUPS, EXT, 128), f32), pltpu.VMEM((GROUPS, EXT, 128), f32)],
        )(*results)
        return new_pressure.reshape(pressure.shape), water.reshape(pressure.shape)

    cells = P("member", "gx", "gy")
    return jax.shard_map(
        body,
        mesh=mesh,
        in_specs=(cells, cells, P(), P(), cells, cells, cells, P("member"), P("member"), P("member"), P("member")),
        out_specs=(cells, cells),
        check_vma=False,
    )
```

time: 184 us -> 60.8 us (0.33); the launches traced: 181 us -> 60.6 us
  starting transfers between devices: 80.3 us -> 0 us
  Pallas kernels: 0 us -> 60 us
  local copies, waits for them, and re-layouts: 45.4 us -> 0 us
  other arithmetic: 43.8 us -> 0 us
  matrix products: 6.35 us -> 0 us
  waiting for transfers between devices: 3.93 us -> 0 us
    ppermute x16 -> x0, starting transfers between devices: 80.3 us -> none  [the longest x4 44.7 us: padded(): lax.ppermute(lax.slice_in_dim(block, 0, width, axis=dim), axis, backward)]
    pallas_call x0 -> x2, Pallas kernels: none -> 60 us  [the longest x1 56 us: body(): pl.pallas_call(lambda *refs: comm_kernel(sizes, *refs), name='exchange',...]
    reshape x9 -> x0, local copies, waits for them, and re-layouts: 17 us -> none  [the longest x8 15 us: to_blocks(): summed = field.reshape(layers // BZ, BZ, span_x, span_y).sum(axis=1)]
    slice x22 -> x0, local copies, waits for them, and re-layouts: 13.4 us -> none  [the longest x11 8.55 us: trim_border(): field[:, border_width:field.shape[1] - border_width, border_width:field.s...]
    reduce_sum x8 -> x0, other arithmetic: 10.9 us -> none  [to_blocks(): summed = field.reshape(layers // BZ, BZ, span_x, span_y).sum(axis=1)]
    mul x19 -> x0, other arithmetic: 10.1 us -> none  [the longest x12 3.5 us: march_forward(): jnp.where(flows[axis] > 0, lower(frac, axis), upper(frac, axis))]
    unnamed x62 -> x0, local copies, waits for them, and re-layouts: 6.62 us -> none
    dot_general x19 -> x0, matrix products: 6.35 us -> none  [the longest x8 1.63 us: to_blocks(): return jnp.einsum('zkb,bl->zkl', partial_sum, own_y, precision=highest)]
  transfers between devices with their start and end apart: 16 -> 0, of which waited for: 2 -> 0; matrix products, arithmetic and copies ran while one was open for 23% -> 0% of each run, Pallas kernels for 0% -> 0%
where the time goes in v1:
time: 60.8 us; the launch traced here: 60.6 us
  Pallas kernels  60 us (99%)
  between operations  0.64 us (1%)
    pallas_call x1, Pallas kernels, body(): pl.pallas_call(lambda *refs: comm_kernel(sizes, *refs), name='exchange',...  56 us
    pallas_call x1, Pallas kernels, body(): pl.pallas_call(transport_kernel, name='transport', out_shape=[shape, shap...  3.93 us

profile of v1, /device:TPU:65, one launch (start us, length us, event | category | flops | bytes accessed | tf_op | source)
XLA Modules:
  0.0 60.6 jit_solution(9784529001550389147)
XLA Ops:
  0.6 56.0 %exchange.1 = (f32[4,136,128]{2,1,0:T(8,128)}, f32[4,136,128]{2,1,0:T(8,128)}, f32[4,136,128]{2,1,0:T(8,128)}, f32[4,136,128]{2,1,0:T(8,128)}, f32[4,136,128]{2,...) custom-call(f32[256,128]{1,0:T(8,128)} %bitcast.10, s32[256,128]{1,0:T(8,128)} %bitcast.11, ...), custom_call_target="tpu_custom_call" | custom-call | tf_op jit(solution)/shard_map/exchange/pallas_call | solution.py:480
  56.7 3.9 %transport.1 = (f32[256,128]{1,0:T(8,128)}, f32[256,128]{1,0:T(8,128)}) custom-call(f32[4,136,128]{2,1,0:T(8,128)} %get-tuple-element.11.fx, f32[4,136,128]{2,1,0:T(8,128)} %get-tuple-element.12.fy, f32[4,136,128]{2,1,0:T(8,128)} %get-tuple-element.13.fz, f32[4,136,128]{2,1,0:T(8,128)} %get-tuple-element.14.s_in, f32[4,136,128]{2,1,0:T(8,128)} %get-tuple-element.15.w, ...), custom_call_target="tpu_custom_call" | custom-call | tf_op jit(solution)/shard_map/transport/pallas_call | solution.py:513

commit v2 on v1

--- a/solution.py
+++ b/solution.py
@@ -20,7 +20,6 @@
 REACH = 4
 
 time_step = 0.005
-MESH = pl.DeviceIdType.MESH
 f32 = jnp.float32
 bf16 = jnp.bfloat16
 M, PR, B, S, PHI = range(5)
@@ -71,9 +70,10 @@
 
 def comm_kernel(
     sizes,
-    perm, fac, pres, sat, bas, bymap, wells, rates, bxmap, fpor, fmob,
-    fx_out, fy_out, fz_out, s_out, w_out, src_out, np_out,
-    mob, por, newp, E, yh, xs, xr, ys, yr, ps, low, high,
+    perm_h, fac_h, pres_h, sat_h, bas_h, bymap_h, wells_h, rates_h, bxmap_h, fpor_h, fmob_h,
+    tx_out, ty_out, tz_out, s_out, w_out, src_out, newp,
+    perm, fac, pres, sat, bas, bymap, wells, rates, bxmap, fpor, fmob, in_sem,
+    mob, por, E, yh, xs, xr, ys, yr, ps, low, high,
     send_a, recv_a, send_h, recv_h, send_c, recv_c,
 ):
     n_gx, n_gy, full_y = sizes
@@ -92,26 +92,47 @@
         return {"gx": gx + dx, "gy": gy + dy}
 
     partners = [(dx, dy) for dx in range(-REACH, REACH + 1) for dy in (-1, 0, 1) if (dx, dy) != (0, 0)]
+    partners.sort(key=lambda d: abs(d[0]) + abs(d[1]))
+    inputs = [
+        pltpu.make_async_copy(src, dst, in_sem.at[i])
+        for i, (src, dst) in enumerate(zip(
+            (sat_h, fac_h, perm_h, fpor_h, fmob_h, pres_h, bas_h, bxmap_h, bymap_h, wells_h, rates_h),
+            (sat, fac, perm, fpor, fmob, pres, bas, bxmap, bymap, wells, rates),
+        ))
+    ]
+    for copy in inputs:
+        copy.start()
 
     at_edge = (gx < REACH) | (gx >= n_gx - REACH) | (gy == 0) | (gy == n_gy - 1)
 
     @pl.when(at_edge)
     def _():
-        xr[...] = jnp.zeros_like(xr)
-        yr[...] = jnp.zeros_like(yr)
-        yh[...] = jnp.zeros_like(yh)
         ps[...] = jnp.zeros_like(ps)
         low[...] = jnp.zeros_like(low)
         high[...] = jnp.zeros_like(high)
+        yh[...] = jnp.zeros_like(yh)
+        yr[...] = jnp.zeros_like(yr)
+
+    @pl.when(gx == 0)
+    def _():
+        xr[0] = jnp.zeros(xr.shape[1:], f32)
         for f in range(5):
             E[f, 0] = jnp.zeros((EXT, 128), f32)
+
+    @pl.when(gx == n_gx - 1)
+    def _():
+        xr[1] = jnp.zeros(xr.shape[1:], f32)
+        for f in range(5):
             E[f, 3] = jnp.zeros((EXT, 128), f32)
 
     barrier = pltpu.get_barrier_semaphore()
     for dx, dy in partners:
         @pl.when(there(dx, dy))
         def _(dx=dx, dy=dy):
-            pl.semaphore_signal(barrier, inc=1, device_id=where_is(dx, dy), device_id_type=MESH)
+            pl.semaphore_signal(barrier, inc=1, device_id=where_is(dx, dy), device_id_type=pl.DeviceIdType.MESH)
+
+    for i in (0, 1, 2, 3, 4):
+        inputs[i].wait()
 
     region = fac[...]
     s_nat = sat[...]
@@ -126,6 +147,9 @@
     def column(ref, x):
         return ref[pl.ds(x, NZ, NXL), :]
 
+    for i in (5, 6):
+        inputs[i].wait()
+
     own_edge = []
     for side, x in ((0, 0), (1, NXL - 1)):
         edge = [column(mob, x), column(pres, x), column(bas, x)]
@@ -133,17 +157,6 @@
         for k in range(3):
             xs[side, NZ * k : NZ * (k + 1), :] = edge[k]
 
-    for f, ref in ((M, mob), (PR, pres), (B, bas), (S, sat), (PHI, por)):
-        for g in (1, 2):
-            block = jnp.concatenate([column(ref, 4 * (g - 1) + i) for i in range(4)], axis=0)
-            E[f, g, 0:NYL, :] = block.T
-
-    ys[...] = jnp.zeros_like(ys)
-    for side, y in ((0, 0), (1, NYL - 1)):
-        for k, f in enumerate((M, PR, B)):
-            for g in (1, 2):
-                ys[side, 2 * k + g - 1 : 2 * k + g, :] = E[f, g, y : y + 1, :]
-
     span_x = lax.min(gx, REACH) + lax.min(n_gx - 1 - gx, REACH) + 1
     span_y = lax.min(gy, 1) + lax.min(n_gy - 1 - gy, 1) + 1
     pl.semaphore_wait(barrier, span_x * span_y - 1)
@@ -153,7 +166,7 @@
             self.dx, self.dy = dx, dy
             self.copy = pltpu.make_async_remote_copy(
                 src_ref=src, dst_ref=dst, send_sem=sends.at[slot_out], recv_sem=recvs.at[slot_in],
-                device_id=where_is(dx, dy), device_id_type=MESH,
+                device_id=where_is(dx, dy), device_id_type=pl.DeviceIdType.MESH,
             )
 
         def start(self):
@@ -171,8 +184,25 @@
         Copy(ys.at[1], yr.at[0], send_a, recv_a, 2, 2, 0, 1),
         Copy(ys.at[0], yr.at[1], send_a, recv_a, 3, 3, 0, -1),
     ]
-    for copy in edges:
+    for copy in edges[:2]:
         copy.start()
+
+    def turn(pairs):
+        for f, ref in pairs:
+            for g in (1, 2):
+                block = jnp.concatenate([column(ref, 4 * (g - 1) + i) for i in range(4)], axis=0)
+                E[f, g, 0:NYL, :] = block.T
+
+    turn(((M, mob), (PR, pres), (B, bas)))
+
+    ys[...] = jnp.zeros_like(ys)
+    for side, y in ((0, 0), (1, NYL - 1)):
+        for k, f in enumerate((M, PR, B)):
+            for g in (1, 2):
+                ys[side, 2 * k + g - 1 : 2 * k + g, :] = E[f, g, y : y + 1, :]
+    for copy in edges[2:]:
+        copy.start()
+    turn(((S, sat), (PHI, por)))
 
     def halo_x(k, fields):
         return [
@@ -194,6 +224,8 @@
     ]
     for copy in halo_early + halo_y:
         copy.start()
+    for i in (7, 8, 9, 10):
+        inputs[i].wait()
 
     well_y = wells[...] % full_y
     well_x = wells[...] // full_y
@@ -380,9 +412,9 @@
     for g in range(GROUPS):
         after = min(g + 1, GROUPS - 1)
         here = E[M, g]
-        fx_out[g] = harmonic(here, next_x(here, E[M, after]))
-        fy_out[g] = harmonic(here, roll(here, -1, 0))
-        fz_out[g] = jnp.where(z_ext < NZ - 1, 0.1 * harmonic(here, roll(here, -1, 1)), 0.0)
+        tx_out[g] = harmonic(here, next_x(here, E[M, after]))
+        ty_out[g] = harmonic(here, roll(here, -1, 0))
+        tz_out[g] = jnp.where(z_ext < NZ - 1, 0.1 * harmonic(here, roll(here, -1, 1)), 0.0)
         s_out[g] = E[S, g]
         phi_here = E[PHI, g]
         w_out[g] = time_step / jnp.where(phi_here > 0, phi_here, 1.0)
@@ -419,48 +451,60 @@
 
     for g in range(GROUPS):
         newp[g] = E[PR, g] + E[B, g] * fine[:, 128 * g : 128 * (g + 1)]
-    for g in range(GROUPS):
-        after = min(g + 1, GROUPS - 1)
-        here = newp[g]
-        fx_out[g] = fx_out[g] * (here - next_x(here, newp[after]))
-        fy_out[g] = fy_out[g] * (here - roll(here, -1, 0))
-        fz_out[g] = fz_out[g] * (here - roll(here, -1, 1))
-        if g in (1, 2):
-            np_out[g - 1] = here[0:NYL]
-
     for copy in edges + halo_early + halo_late + halo_y + coarse:
         copy.wait_send()
 
 
-def transport_kernel(fx, fy, fz, s_in, w, src, np_in, np_out, s_out, s, out_x):
+def transport_kernel(tx, ty, tz, s_in, w_in, src, newp, np_out, s_out, s, F, fx, C):
+    first, last_row = 8, 8 + EXT - 1
+
+    def flows(g):
+        after = min(g + 1, GROUPS - 1)
+        return newp[g] - next_x(newp[g], newp[after])
+
     for g in range(GROUPS):
-        s[g] = s_in[g]
+        fx[g] = tx[g] * flows(g)
+    for g in range(GROUPS):
+        here = newp[g]
+        w = w_in[g]
+        source = src[g]
+        fx_up = fx[g]
+        fx_down = prev_x(fx_up, fx[max(g - 1, 0)])
+        fy_up = ty[g] * (here - roll(here, -1, 0))
+        fy_down = roll(fy_up, 1, 0)
+        fz_up = tz[g] * (here - roll(here, -1, 1))
+        fz_down = roll(fz_up, 1, 1)
+        C[0, g] = w * jnp.maximum(source, 0.0)
+        leaves = jnp.minimum(source, 0.0)
+        for k, (up, down) in enumerate(((fx_up, fx_down), (fy_up, fy_down), (fz_up, fz_down))):
+            from_up = jnp.maximum(-up, 0.0)
+            from_down = jnp.maximum(down, 0.0)
+            C[2 + 2 * k, g] = w * from_up
+            C[3 + 2 * k, g] = w * from_down
+            leaves = leaves - (up + from_up) + (down - from_down)
+        C[1, g] = w * leaves
+
     for step in range(NSUB):
-        last = step == NSUB - 1
-        frac = []
+        groups = (1, 2) if step == NSUB - 1 else range(GROUPS)
         for g in range(GROUPS):
-            v = s[g]
+            v = s_in[g] if step == 0 else s[g]
             wet = v * v
-            frac.append(wet / (wet + (1.0 - v) * (1.0 - v) * 0.25))
-        carried = []
-        for g in range(GROUPS):
-            flow = fx[g]
-            after = frac[min(g + 1, GROUPS - 1)]
-            carried.append(jnp.where(flow > 0, frac[g], next_x(frac[g], after)) * flow)
-        for g in range(GROUPS):
-            if last and g in (0, 3):
-                continue
-            flow = fy[g]
-            cy = jnp.where(flow > 0, frac[g], roll(frac[g], -1, 0)) * flow
-            flow = fz[g]
-            cz = jnp.where(flow > 0, frac[g], roll(frac[g], -1, 1)) * flow
-            cx = carried[g]
-            out = cx - prev_x(cx, carried[max(g - 1, 0)]) + cy - roll(cy, 1, 0) + cz - roll(cz, 1, 1)
-            source = src[g]
-            change = jnp.maximum(source, 0.0) + jnp.minimum(source, 0.0) * frac[g] - out
-            s[g] = s[g] + w[g] * change
+            f = wet / (wet + (1.0 - v) * (1.0 - v) * 0.25)
+            F[g, first : first + EXT] = f
+            F[g, first - 1 : first] = f[EXT - 1 : EXT]
+            F[g, last_row + 1 : last_row + 2] = f[0:1]
+        for g in groups:
+            f = F[g, first : first + EXT]
+            f_after = F[min(g + 1, GROUPS - 1), first : first + EXT]
+            f_before = F[max(g - 1, 0), first : first + EXT]
+            v = s_in[g] if step == 0 else s[g]
+            v = v + C[0, g] + C[1, g] * f
+            v = v + C[4, g] * F[g, first + 1 : first + 1 + EXT] + C[5, g] * F[g, first - 1 : first - 1 + EXT]
+            v = v + C[2, g] * next_x(f, f_after) + C[3, g] * prev_x(f, f_before)
+            v = v + C[6, g] * roll(f, -1, 1) + C[7, g] * roll(f, 1, 1)
+            s[g] = v
     for g in (1, 2):
-        for block, dst in ((s[g, 0:NYL, :], s_out), (np_in[g - 1], np_out)):
+        for block, dst in ((s[g, 0:NYL, :], s_out), (newp[g, 0:NYL, :], np_out)):
             back = block.T
             for i in range(4):
                 dst[pl.ds(4 * (g - 1) + i, NZ, NXL), :] = back[NZ * i : NZ * (i + 1)]
@@ -469,24 +513,31 @@
 def solution(mesh):
     n_gx, n_gy = mesh.shape["gx"], mesh.shape["gy"]
     vmem = pl.BlockSpec(memory_space=pltpu.VMEM)
-    smem = pl.BlockSpec(memory_space=pltpu.SMEM)
 
     def body(perm, facies, fpor, fmob, pressure, saturation, basis, bx_map, by_map, well_cells, well_rates):
         assert pressure.shape == (NZ, NXL, NYL)
         flat = lambda a: a.reshape(NZ * NXL, NYL)
         sizes = (n_gx, n_gy, by_map.shape[0])
-        wide = jax.ShapeDtypeStruct((GROUPS, EXT, 128), f32)
-        own = jax.ShapeDtypeStruct((2, NYL, 128), f32)
+        wide = pltpu.VMEM((GROUPS, EXT, 128), f32)
+        cells_in = lambda kind=f32: pltpu.VMEM((NZ * NXL, NYL), kind)
+        anywhere = pl.BlockSpec(memory_space=pl.ANY)
         results = pl.pallas_call(
             lambda *refs: comm_kernel(sizes, *refs),
             name="exchange",
-            out_shape=[wide] * 6 + [own],
-            in_specs=[vmem] * 8 + [smem] * 3,
+            out_shape=[wide] * 7,
+            in_specs=[anywhere] * 11,
             out_specs=[vmem] * 7,
             scratch_shapes=[
-                pltpu.VMEM((NZ * NXL, NYL), f32),
-                pltpu.VMEM((NZ * NXL, NYL), f32),
-                pltpu.VMEM((GROUPS, EXT, 128), f32),
+                cells_in(), cells_in(jnp.int32), cells_in(), cells_in(), cells_in(),
+                pltpu.VMEM((n_gy, NYL), jnp.int32),
+                pltpu.VMEM((1, well_cells.shape[0]), jnp.int32),
+                pltpu.VMEM((1, well_cells.shape[0]), f32),
+                pltpu.SMEM(bx_map.shape, jnp.int32),
+                pltpu.SMEM(fpor.shape, f32),
+                pltpu.SMEM(fmob.shape, f32),
+                pltpu.SemaphoreType.DMA((11,)),
+                cells_in(),
+                cells_in(),
                 pltpu.VMEM((5, GROUPS, EXT, 128), f32),
                 pltpu.VMEM((2, 5, GROUPS, 8, 128), f32),
                 pltpu.VMEM((2, 3 * NZ, NYL), f32),
@@ -516,8 +567,13 @@
             out_shape=[shape, shape],
             in_specs=[vmem] * 7,
             out_specs=[vmem] * 2,
-            scratch_shapes=[pltpu.VMEM((GROUPS, EXT, 128), f32), pltpu.VMEM((GROUPS, EXT, 128), f32)],
-        )(*results)
+            scratch_shapes=[
+                pltpu.VMEM((GROUPS, EXT, 128), f32),
+                pltpu.VMEM((GROUPS, EXT + 16, 128), f32),
+                pltpu.VMEM((GROUPS, EXT, 128), f32),
+                pltpu.VMEM((8, GROUPS, EXT, 128), f32),
+            ],
+        )(*[pltpu.with_memory_space_constraint(r, pltpu.VMEM) for r in results])
         return new_pressure.reshape(pressure.shape), water.reshape(pressure.shape)
 
     cells = P("member", "gx", "gy")

time: 60.8 us -> 57.3 us (0.942)
  Pallas kernels: 60 us -> 56.6 us
    pallas_call x1, Pallas kernels: 56 us -> 53.5 us  [body(): pl.pallas_call(lambda *refs: comm_kernel(sizes, *refs), name='exchange',...]
    pallas_call x1, Pallas kernels: 3.93 us -> 3.07 us  [body(): pl.pallas_call(transport_kernel, name='transport', out_shape=[shape, shap...]
where the time goes in v2:
time: 57.3 us; the launch traced here: 57.2 us
  Pallas kernels  56.6 us (99%)
  between operations  0.64 us (1%)
    pallas_call x1, Pallas kernels, body(): pl.pallas_call(lambda *refs: comm_kernel(sizes, *refs), name='exchange',...  53.5 us
    pallas_call x1, Pallas kernels, body(): pl.pallas_call(transport_kernel, name='transport', out_shape=[shape, shap...  3.07 us

profile of v2, /device:TPU:65, one launch (start us, length us, event | category | flops | bytes accessed | tf_op | source)
XLA Modules:
  0.0 57.2 jit_solution(5190908143497002774)
XLA Ops:
  0.6 53.5 %exchange.1 = (f32[4,136,128]{2,1,0:T(8,128)S(1)}, f32[4,136,128]{2,1,0:T(8,128)S(1)}, f32[4,136,128]{2,1,0:T(8,128)S(1)}, f32[4,136,128]{2,1,0:T(8,128)S(1)}, f...) custom-call(f32[256,128]{1,0:T(8,128)} %bitcast.10, s32[256,128]{1,0:T(8,128)} %bitcast.11, ...), custom_call_target="tpu_custom_call" | custom-call | tf_op jit(solution)/shard_map/exchange/pallas_call | solution.py:524
  54.1 3.1 %transport.1 = (f32[256,128]{1,0:T(8,128)}, f32[256,128]{1,0:T(8,128)}) custom-call(f32[4,136,128]{2,1,0:T(8,128)S(1)} %get-tuple-element.11.tx, f32[4,136,128]{2,1,0:T(8,128)S(1)} %get-tuple-element.12.ty, f32[4,136,128]{2,1,0:T(8,128)S(1)} %get-tuple-element.13.tz, f32[4,136,128]{2,1,0:T(8,128)S(1)} %get-tuple-element.14.s_in, ...), custom_call_target="tpu_custom_call" | custom-call | tf_op jit(solution)/shard_map/transport/pallas_call | solution.py:564

commit v3 on v2

v3 whole, which is shorter than its diff:
```python
import jax
import jax.numpy as jnp
from jax import lax
from jax.experimental import pallas as pl
from jax.experimental.pallas import tpu as pltpu
from jax.sharding import PartitionSpec as P

NZ = 32
BX = 8
BY = 8
BZ = 4
NSWEEP = 3
NSUB = 4
NFAC = 4
NXL = 8
NYL = 128
EXT = NYL + 8
GROUPS = 4
ROWS_C = 24
REACH = 4

time_step = 0.005
f32 = jnp.float32
bf16 = jnp.bfloat16
M, PR, B, S, PHI = range(5)


def iota(shape, dim):
    return lax.broadcasted_iota(jnp.int32, shape, dim)


def harmonic(left, right):
    total = left + right
    return 2.0 * left * right / jnp.where(total > 0, total, 1.0)


def split2(v):
    hi = v.astype(bf16)
    return hi, (v - hi.astype(f32)).astype(bf16)


def split3(v):
    hi = v.astype(bf16)
    rest = v - hi.astype(f32)
    mid = rest.astype(bf16)
    return hi, mid, (rest - mid.astype(f32)).astype(bf16)


def nn(a, b):
    return lax.dot_general(a, b, (((1,), (0,)), ((), ())), preferred_element_type=f32)


def nt(a, b):
    return lax.dot_general(a, b, (((1,), (1,)), ((), ())), preferred_element_type=f32)


def roll(v, shift, axis):
    return pltpu.roll(v, shift % v.shape[axis], axis)


def next_x(here, after):
    lane = iota(here.shape, 1)
    return jnp.where(lane < 96, roll(here, -32, 1), roll(after, -32, 1))


def prev_x(here, before):
    lane = iota(here.shape, 1)
    return jnp.where(lane >= 32, roll(here, 32, 1), roll(before, 32, 1))


def fetch_properties(perm, fac, sat, fpor, fmob, mob, por):
    region = fac[...]
    s_nat = sat[...]
    fm = jnp.zeros(region.shape, f32)
    fp = jnp.zeros(region.shape, f32)
    for level in range(NFAC):
        fm = jnp.where(region == level, fmob[level], fm)
        fp = jnp.where(region == level, fpor[level], fp)
    mob[...] = perm[...] * fm * (s_nat * s_nat + (1.0 - s_nat) * (1.0 - s_nat) * 0.25)
    por[...] = fp


def turned(ref, g):
    block = jnp.concatenate([ref[pl.ds(4 * (g - 1) + i, NZ, NXL), :] for i in range(4)], axis=0)
    return block.T


def edge_rows(ref, x):
    return jnp.concatenate([ref[pl.ds(x + NXL * i, NZ // BZ, NXL * BZ), :] for i in range(BZ)], axis=0)


class Copy:
    def __init__(self, src, dst, send, recv, target, goes, comes):
        self.goes, self.comes = goes, comes
        self.copy = pltpu.make_async_remote_copy(
            src_ref=src, dst_ref=dst, send_sem=send, recv_sem=recv, device_id=target, device_id_type=pl.DeviceIdType.MESH
        )

    def start(self):
        pl.when(self.goes)(lambda: self.copy.start())

    def wait_send(self):
        pl.when(self.goes)(lambda: self.copy.wait_send())

    def wait_recv(self):
        pl.when(self.comes)(lambda: self.copy.wait_recv())


def pair_kernel(
    n_gx, perm_h, fac_h, pres_h, sat_h, bas_h, fpor_h, fmob_h, block_out, edge_out,
    perm, fac, pres, sat, bas, fpor, fmob, in_sem, mob, por, block, edge, block_in, edge_in, send, recv,
):
    gx = lax.axis_index("gx")
    odd = gx % 2 == 1
    partner = jnp.where(odd, gx + 1, gx - 1)
    linked = (partner >= 0) & (partner < n_gx)
    barrier = pltpu.get_barrier_semaphore()

    @pl.when(jnp.logical_not(linked))
    def _():
        block_out[...] = jnp.zeros_like(block_out)
        edge_out[...] = jnp.zeros_like(edge_out)

    @pl.when(linked)
    def _():
        inputs = [
            pltpu.make_async_copy(src, dst, in_sem.at[i])
            for i, (src, dst) in enumerate(zip(
                (sat_h, fac_h, perm_h, fpor_h, fmob_h, pres_h, bas_h), (sat, fac, perm, fpor, fmob, pres, bas)
            ))
        ]
        for copy in inputs:
            copy.start()
        pl.semaphore_signal(barrier, inc=1, device_id={"gx": partner}, device_id_type=pl.DeviceIdType.MESH)
        for copy in inputs:
            copy.wait()
        fetch_properties(perm, fac, sat, fpor, fmob, mob, por)

        def fill(g, x):
            for f, ref in ((M, mob), (PR, pres), (B, bas), (S, sat), (PHI, por)):
                block[f] = turned(ref, g)
            for k, ref in enumerate((mob, pres, bas)):
                edge[NZ * k : NZ * (k + 1)] = edge_rows(ref, x)

        pl.when(odd)(lambda: fill(2, NXL - 1))
        pl.when(jnp.logical_not(odd))(lambda: fill(1, 0))
        pl.semaphore_wait(barrier, 1)
        copies = [
            pltpu.make_async_remote_copy(
                src_ref=src, dst_ref=dst, send_sem=send.at[i], recv_sem=recv.at[i],
                device_id={"gx": partner}, device_id_type=pl.DeviceIdType.MESH,
            )
            for i, (src, dst) in enumerate(((edge, edge_in), (block, block_in)))
        ]
        for copy in copies:
            copy.start()
        for copy in copies:
            copy.wait()
        block_out[...] = block_in[...]
        edge_out[...] = edge_in[...]


def comm_kernel(
    sizes,
    perm, fac, pres, sat, bas, block_in, edge_in, bymap_h, wells_h, rates_h, bxmap_h, fpor_h, fmob_h,
    tx_out, ty_out, tz_out, s_out, w_out, src_out, newp,
    bymap, wells, rates, bxmap, fpor, fmob, in_sem,
    mob, por, E, yh, xs, xr, ys, yr, ps, low, high,
    send_a, recv_a, send_h, recv_h, send_c, recv_c,
):
    n_gx, n_gy, full_y = sizes
    gx = lax.axis_index("gx")
    gy = lax.axis_index("gy")
    odd = gx % 2 == 1
    even = jnp.logical_not(odd)

    def there(dx, dy):
        ok = jnp.bool_(True)
        if dx:
            ok = ok & (gx + dx >= 0) & (gx + dx < n_gx)
        if dy:
            ok = ok & (gy + dy >= 0) & (gy + dy < n_gy)
        return ok

    def where_is(dx, dy):
        return {"gx": gx + dx, "gy": gy + dy}

    partners = [(dx, dy) for dx in range(-REACH, REACH + 1) for dy in (-1, 0, 1) if (dx, dy) != (0, 0)]
    partners.sort(key=lambda d: abs(d[0]) + abs(d[1]))

    inputs = [
        pltpu.make_async_copy(src, dst, in_sem.at[i])
        for i, (src, dst) in enumerate(zip(
            (fpor_h, fmob_h, bxmap_h, bymap_h, wells_h, rates_h), (fpor, fmob, bxmap, bymap, wells, rates)
        ))
    ]
    for copy in inputs:
        copy.start()

    at_edge = (gx < REACH) | (gx >= n_gx - REACH) | (gy == 0) | (gy == n_gy - 1)

    @pl.when(at_edge)
    def _():
        ps[...] = jnp.zeros_like(ps)
        low[...] = jnp.zeros_like(low)
        high[...] = jnp.zeros_like(high)
        yh[...] = jnp.zeros_like(yh)
        yr[...] = jnp.zeros_like(yr)

    barrier = pltpu.get_barrier_semaphore()
    for dx, dy in partners:
        @pl.when(there(dx, dy))
        def _(dx=dx, dy=dy):
            pl.semaphore_signal(barrier, inc=1, device_id=where_is(dx, dy), device_id_type=pl.DeviceIdType.MESH)

    for copy in inputs[:2]:
        copy.wait()
    fetch_properties(perm, fac, sat, fpor, fmob, mob, por)

    def turn(pairs):
        for f, ref in pairs:
            for g in (1, 2):
                E[f, g, 0:NYL, :] = turned(ref, g)

    turn(((M, mob), (PR, pres), (B, bas)))
    ys[...] = jnp.zeros_like(ys)
    for side, y in ((0, 0), (1, NYL - 1)):
        for k, f in enumerate((M, PR, B)):
            for g in (1, 2):
                ys[side, 2 * k + g - 1 : 2 * k + g, :] = E[f, g, y : y + 1, :]
    own_edge = []
    for x in (0, NXL - 1):
        own_edge.append([edge_rows(ref, x) for ref in (mob, pres, bas)])
    for k in range(3):
        xs[NZ * k : NZ * (k + 1)] = jnp.where(odd, own_edge[0][k], own_edge[1][k])

    span_x = lax.min(gx, REACH) + lax.min(n_gx - 1 - gx, REACH) + 1
    span_y = lax.min(gy, 1) + lax.min(n_gy - 1 - gy, 1) + 1
    pl.semaphore_wait(barrier, span_x * span_y - 1)

    def to(src, dst, sends, recvs, slot_out, slot_in, dx, dy):
        return Copy(src, dst, sends.at[slot_out], recvs.at[slot_in], where_is(dx, dy), there(dx, dy), there(-dx, -dy))

    mate = {"gx": jnp.where(odd, gx - 1, gx + 1)}
    always = jnp.bool_(True)
    edges = [
        to(ys.at[1], yr.at[0], send_a, recv_a, 2, 2, 0, 1),
        to(ys.at[0], yr.at[1], send_a, recv_a, 3, 3, 0, -1),
        Copy(xs, xr, send_a.at[0], recv_a.at[0], mate, always, always),
    ]
    for copy in edges:
        copy.start()
    turn(((S, sat), (PHI, por)))

    up, down = slice(NYL - 8, NYL), slice(0, 8)
    every = slice(0, 5)
    halo = [
        to(E.at[every, 1:3, up], yh.at[0, every, 1:3], send_h, recv_h, 4, 4, 0, 1),
        to(E.at[every, 1:3, down], yh.at[1, every, 1:3], send_h, recv_h, 5, 5, 0, -1),
        to(E.at[every, 2, up], yh.at[0, every, 0], send_h, recv_h, 6, 6, 1, 1),
        to(E.at[every, 1, up], yh.at[0, every, 3], send_h, recv_h, 7, 7, -1, 1),
        to(E.at[every, 2, down], yh.at[1, every, 0], send_h, recv_h, 8, 8, 1, -1),
        to(E.at[every, 1, down], yh.at[1, every, 3], send_h, recv_h, 9, 9, -1, -1),
        Copy(E.at[every, 2, 0:NYL], E.at[every, 0, 0:NYL], send_h.at[0], recv_h.at[0], mate, even, odd),
        Copy(E.at[every, 1, 0:NYL], E.at[every, 3, 0:NYL], send_h.at[1], recv_h.at[1], mate, odd, even),
    ]
    for copy in halo:
        copy.start()
    for copy in inputs[2:]:
        copy.wait()

    @pl.when(even)
    def _():
        E[every, 0, 0:NYL] = block_in[...]

    @pl.when(odd)
    def _():
        E[every, 3, 0:NYL] = block_in[...]

    well_y = wells[...] % full_y
    well_x = wells[...] // full_y
    n_wells = wells.shape[1]
    row = iota((EXT, 1), 0)
    y_here = gy * NYL + jnp.where(row < NYL + 4, row, row - EXT)
    hits_y = (y_here == well_y).astype(f32).astype(bf16)
    x_here = gx * NXL - 4 + iota((16, 1), 0)
    hits_x = jnp.where(x_here == well_x, rates[...], 0.0)
    col = nt(hits_y, jnp.concatenate(split3(hits_x), axis=0))
    col = (col[:, 0:16] + col[:, 16:32] + col[:, 32:48]) * (1.0 / NZ)
    lane = iota((16, 512), 1)
    spread = (lane // NZ == iota((16, 512), 0)).astype(f32).astype(bf16)
    src = nn(jnp.concatenate(split3(col), axis=1), jnp.concatenate([spread] * 3, axis=0))
    for g in range(GROUPS):
        src_out[g] = src[:, 128 * g : 128 * (g + 1)]

    blocks_y = NYL // BY
    map_own = bymap[pl.ds(gy, 1), :] - (gy * blocks_y - 4)
    map_up = bymap[pl.ds(lax.min(gy + 1, n_gy - 1), 1), :] - (gy * blocks_y - 4)
    map_down = bymap[pl.ds(lax.max(gy - 1, 0), 1), :] - (gy * blocks_y - 4)
    sum_y = (iota((ROWS_C, NYL), 0) == map_own).astype(f32).astype(bf16)
    sum_y = jnp.concatenate([sum_y, sum_y], axis=1)

    def column_of(values):
        return jnp.broadcast_to(values.astype(f32), (128, 128)).T

    by_row = column_of(map_own)
    by_up = column_of(map_up)[0:8]
    by_down = column_of(map_down)[120:128]
    by_ext = jnp.concatenate([by_row, jnp.where(iota((8, 128), 0) < 4, by_up, by_down)], axis=0)
    spread_y = (by_ext[:, 0:ROWS_C] == iota((EXT, ROWS_C), 1).astype(f32)).astype(f32).astype(bf16)
    same_y = (by_row == jnp.concatenate([by_row[1:], by_row[:1]], axis=0)).astype(f32)

    kx = [bxmap[lax.clamp(0, gx * NXL - 4 + i, n_gx * NXL - 1)] - gx for i in range(16)]

    def lanes_of(values, shape):
        which = iota(shape, 1) // NZ
        total = jnp.zeros(shape, jnp.int32)
        for i, value in enumerate(values):
            total = jnp.where(which == i, value, total)
        return total

    z_block = (iota((1, 256), 1) % NZ) // BZ
    target = (lanes_of(kx[4:12], (1, 256)) + 1) * 8 + z_block
    sum_xz = (iota((128, 256), 0) == target).astype(f32).astype(bf16)
    sum_xz = jnp.concatenate([sum_xz, sum_xz], axis=1)

    lane128 = iota((NYL, 128), 1)
    row128 = iota((NYL, 128), 0)
    z_of = lane128 % NZ
    m = [E[M, g, 0:NYL, :] for g in (1, 2)]
    p = [E[PR, g, 0:NYL, :] for g in (1, 2)]
    b = [E[B, g, 0:NYL, :] for g in (1, 2)]
    phi = [E[PHI, g, 0:NYL, :] for g in (1, 2)]
    own_src = [src[0:NYL, 128 * g : 128 * (g + 1)] for g in (1, 2)]
    same_x = [lanes_of([(kx[4 + 4 * g + i] == kx[5 + 4 * g + i]).astype(jnp.int32) for i in range(4)], (1, 128)) for g in (0, 1)]

    def nx_(v, g):
        return next_x(v[0], v[1]) if g == 0 else roll(v[1], -32, 1)

    def ny_(v):
        return roll(v, -1, 0)

    def nz_(v):
        return roll(v, -1, 1)

    tx = [harmonic(m[0], nx_(m, 0)), jnp.where(lane128 < 96, harmonic(m[1], nx_(m, 1)), 0.0)]
    ty = [jnp.where(row128 < NYL - 1, harmonic(v, ny_(v)), 0.0) for v in m]
    tz = [jnp.where(z_of < NZ - 1, 0.1 * harmonic(v, nz_(v)), 0.0) for v in m]
    qx = [tx[g] * (p[g] - nx_(p, g)) for g in (0, 1)]
    sums = []
    for g in (0, 1):
        qy = ty[g] * (p[g] - ny_(p[g]))
        qz = tz[g] * (p[g] - nz_(p[g]))
        in_x = prev_x(qx[g], qx[0]) if g == 1 else jnp.where(lane128 >= 32, roll(qx[0], 32, 1), 0.0)
        t_in_x = prev_x(tx[g], tx[0]) if g == 1 else jnp.where(lane128 >= 32, roll(tx[0], 32, 1), 0.0)
        out = qx[g] - in_x + qy - roll(qy, 1, 0) + qz - roll(qz, 1, 1)
        resid = b[g] * (own_src[g] - out)
        cond = tx[g] + t_in_x + ty[g] + roll(ty[g], 1, 0) + tz[g] + roll(tz[g], 1, 1)
        cx = tx[g] * b[g] * nx_(b, g)
        cy = ty[g] * b[g] * ny_(b[g])
        cz = tz[g] * b[g] * nz_(b[g])
        keep_x = same_x[g].astype(f32)
        keep_z = (z_of % BZ != BZ - 1).astype(f32)
        diag = b[g] * b[g] * (0.5 * phi[g] + cond) - 2.0 * (cx * keep_x + cy * same_y + cz * keep_z)
        sums.append((resid, diag, cz * (1.0 - keep_z), cx * (1.0 - keep_x), cy * (1.0 - same_y)))
    inner = []
    for q in range(5):
        hi, mid = split2(jnp.concatenate([sums[0][q], sums[1][q]], axis=1))
        inner.append(nn(sum_y, jnp.concatenate([hi, mid], axis=0)))

    k_low, k_high, k_next = kx[4], kx[11], kx[12]
    together = k_high == k_next
    for copy in edges:
        copy.wait_recv()

    from_mate = [xr[NZ * k : NZ * (k + 1)] for k in range(3)]
    from_link = [edge_in[NZ * k : NZ * (k + 1)] for k in range(3)]
    m0, p0, b0 = [jnp.where(odd, v, w) for v, w in zip(from_mate, from_link)]
    m1, p1, b1 = [jnp.where(odd, w, v) for v, w in zip(from_mate, from_link)]
    (om0, op0, ob0), (om1, op1, ob1) = own_edge
    t1 = harmonic(om1, m1)
    t0 = harmonic(om0, m0)

    def layers(v):
        return v[0:8] + v[8:16] + v[16:24] + v[24:32]

    r1, d1, c1 = layers(-ob1 * t1 * (op1 - p1)), layers(ob1 * ob1 * t1), layers(ob1 * b1 * t1)
    r0, d0 = layers(-ob0 * t0 * (op0 - p0)), layers(ob0 * ob0 * t0)
    nothing = jnp.zeros((8, 128), f32)
    d1 = d1 - 2.0 * jnp.where(together, c1, nothing)
    c1 = jnp.where(together, nothing, c1)
    placed = []
    for high_part, low_part in ((r1, r0), (d1, d0), (nothing, nothing), (c1, nothing), (nothing, nothing)):
        for k in (-1, 0, 1):
            placed.append(jnp.where(k_high == k, high_part, nothing) + jnp.where(k_low == k, low_part, nothing))
    hi, mid = split2(jnp.concatenate(placed + [nothing], axis=0))
    mine = nt(sum_y, jnp.concatenate([hi, mid], axis=1))

    def wide(ref, side, k):
        return jnp.concatenate([ref[side, 2 * k : 2 * k + 1, :], ref[side, 2 * k + 1 : 2 * k + 2, :]], axis=1)

    um, up_, ub = [wide(yr, 1, k) for k in range(3)]
    dm, dp, db = [wide(yr, 0, k) for k in range(3)]
    om1, op1, ob1 = [wide(ys, 1, k) for k in range(3)]
    om0, op0, ob0 = [wide(ys, 0, k) for k in range(3)]
    t1 = harmonic(om1, um)
    t0 = harmonic(om0, dm)
    rows = iota((ROWS_C, 1), 0)
    r_high = by_row[NYL - 1 : NYL, 0:1].astype(jnp.int32)
    r_low = by_row[0:1, 0:1].astype(jnp.int32)
    r_next = by_up[0:1, 0:1].astype(jnp.int32)
    at_high = rows == r_high
    at_low = rows == r_low
    same = r_high == r_next
    couple = ob1 * ub * t1
    zero = jnp.zeros_like(couple)
    inner[0] = inner[0] + jnp.where(at_high, -ob1 * t1 * (op1 - up_), 0.0) + jnp.where(at_low, -ob0 * t0 * (op0 - dp), 0.0)
    inner[1] = (
        inner[1] + jnp.where(at_high, ob1 * ob1 * t1 - 2.0 * jnp.where(same, couple, zero), 0.0)
        + jnp.where(at_low, ob0 * ob0 * t0, 0.0)
    )
    inner[4] = inner[4] + jnp.where(at_high, jnp.where(same, zero, couple), 0.0)
    hi, mid = split2(jnp.concatenate(inner, axis=0))
    partial = nt(jnp.concatenate([hi, mid], axis=1), sum_xz)
    for q in range(5):
        mine = mine + roll(partial[ROWS_C * q : ROWS_C * (q + 1)], 24 * q, 1)
    ps[REACH] = mine

    def slot(dx):
        return REACH + dx

    coarse = {}
    for dx in range(-REACH, REACH + 1):
        if dx:
            coarse[dx, 0] = to(ps.at[slot(0)], ps.at[slot(-dx)], send_c, recv_c, slot(dx), slot(-dx), dx, 0)
        coarse[dx, 1] = to(
            ps.at[slot(0), 16:24], low.at[slot(-dx)], send_c, recv_c, 9 + slot(dx), 9 + slot(-dx), dx, 1
        )
        coarse[dx, -1] = to(
            ps.at[slot(0), 0:8], high.at[slot(-dx)], send_c, recv_c, 18 + slot(dx), 18 + slot(-dx), dx, -1
        )
    for dx in (4, -4, 3, -3, 2, -2, 1, -1, 0):
        for dy in (1, -1, 0):
            if (dx, dy) in coarse:
                coarse[dx, dy].start()

    target = (lanes_of(kx, (1, 512)) + 3) * 8 + (iota((1, 512), 1) % NZ) // BZ
    spread_xz = (iota((64, 512), 0) == target).astype(f32).astype(bf16)
    spread_xz = jnp.concatenate([spread_xz] * 3, axis=0)

    for copy in halo:
        copy.wait_recv()
    take_up = iota((8, 128), 0) < 4
    for f in range(5):
        for g in range(GROUPS):
            E[f, g, NYL:EXT, :] = jnp.where(take_up, yh[1, f, g], yh[0, f, g])

    z_ext = iota((EXT, 128), 1) % NZ
    for g in range(GROUPS):
        after = min(g + 1, GROUPS - 1)
        here = E[M, g]
        tx_out[g] = harmonic(here, next_x(here, E[M, after]))
        ty_out[g] = harmonic(here, roll(here, -1, 0))
        tz_out[g] = jnp.where(z_ext < NZ - 1, 0.1 * harmonic(here, roll(here, -1, 1)), 0.0)
        s_out[g] = E[S, g]
        phi_here = E[PHI, g]
        w_out[g] = time_step / jnp.where(phi_here > 0, phi_here, 1.0)

    lane24 = iota((ROWS_C, 128), 1)
    system = [jnp.zeros((ROWS_C, 128), f32) for _ in range(5)]
    for dx in sorted(range(-REACH, REACH + 1), key=abs):
        for dy in (-1, 0, 1):
            if (dx, dy) in coarse:
                coarse[-dx, -dy].wait_recv()
        k = slot(dx)
        part = jnp.concatenate([ps[k, 0:8] + low[k], ps[k, 8:16], ps[k, 16:24] + high[k]], axis=0)
        first = (dx + 2) * 8
        take = (lane24 >= max(first, 0)) & (lane24 < min(first + 24, 56))
        for q in range(5):
            system[q] = system[q] + jnp.where(take, roll(part, first - 24 * q, 1), 0.0)
    resid, diag, cz, cx, cy = system
    diag = jnp.where(diag > 0, diag, 1.0)
    half = 0.5 / diag
    fixed = half * resid
    estimate = fixed
    for _ in range(NSWEEP - 1):
        flow = (
            cz * roll(estimate, -1, 1) + roll(cz * estimate, 1, 1)
            + cx * roll(estimate, -8, 1) + roll(cx * estimate, 8, 1)
            + cy * roll(estimate, -1, 0) + roll(cy * estimate, 1, 0)
        )
        estimate = 0.5 * estimate + fixed + half * flow
    row24 = iota((ROWS_C, 128), 0)
    wanted = (row24 >= 3) & (row24 < 21) & (lane24 >= 16) & (lane24 < 40)
    estimate = jnp.where(wanted, estimate, 0.0)[:, 0:64]
    spread1 = nn(jnp.concatenate(split3(estimate), axis=1), spread_xz)
    fine = nn(jnp.concatenate([spread_y] * 3, axis=1), jnp.concatenate(split3(spread1), axis=0))

    for g in range(GROUPS):
        newp[g] = E[PR, g] + E[B, g] * fine[:, 128 * g : 128 * (g + 1)]
    for copy in edges + halo + list(coarse.values()):
        copy.wait_send()


def transport_kernel(tx, ty, tz, s_in, w_in, src, newp, np_out, s_out, s, F, C, np_nat, s_nat, sem):
    first, last_row = 8, 8 + EXT - 1
    lane = iota((EXT, 128), 1)

    def to_next(rolled, g):
        return jnp.where(lane < 96, rolled[g], rolled[min(g + 1, GROUPS - 1)])

    def to_prev(rolled, g):
        return jnp.where(lane >= 32, rolled[g], rolled[max(g - 1, 0)])

    def put(block, g, dst):
        back = block.T
        for i in range(4):
            dst[pl.ds(4 * (g - 1) + i, NZ, NXL), :] = back[NZ * i : NZ * (i + 1)]

    for g in (1, 2):
        put(newp[g, 0:NYL, :], g, np_nat)
    np_copy = pltpu.make_async_copy(np_nat, np_out, sem.at[0])
    np_copy.start()

    rolled = [roll(newp[g], -32, 1) for g in range(GROUPS)]
    fx = [tx[g] * (newp[g] - to_next(rolled, g)) for g in range(GROUPS)]
    rolled = [roll(v, 32, 1) for v in fx]
    for g in range(GROUPS):
        here = newp[g]
        w = w_in[g]
        source = src[g]
        fx_up = fx[g]
        fx_down = to_prev(rolled, g)
        fy_up = ty[g] * (here - roll(here, -1, 0))
        fy_down = roll(fy_up, 1, 0)
        fz_up = tz[g] * (here - roll(here, -1, 1))
        fz_down = roll(fz_up, 1, 1)
        C[0, g] = w * jnp.maximum(source, 0.0)
        leaves = jnp.minimum(source, 0.0)
        for k, (up, down) in enumerate(((fx_up, fx_down), (fy_up, fy_down), (fz_up, fz_down))):
            from_up = jnp.maximum(-up, 0.0)
            from_down = jnp.maximum(down, 0.0)
            C[2 + 2 * k, g] = w * from_up
            C[3 + 2 * k, g] = w * from_down
            leaves = leaves - (up + from_up) + (down - from_down)
        C[1, g] = w * leaves

    for step in range(NSUB):
        last = step == NSUB - 1
        for g in range(GROUPS):
            v = s_in[g] if step == 0 else s[g]
            wet = v * v
            f = wet / (wet + (1.0 - v) * (1.0 - v) * 0.25)
            F[g, first : first + EXT] = f
            F[g, first - 1 : first] = f[EXT - 1 : EXT]
            F[g, last_row + 1 : last_row + 2] = f[0:1]
        ups = [roll(F[g, first : first + EXT], -32, 1) if g or not last else None for g in range(GROUPS)]
        downs = [roll(F[g, first : first + EXT], 32, 1) if g < 3 or not last else None for g in range(GROUPS)]
        for g in (1, 2) if last else range(GROUPS):
            f = F[g, first : first + EXT]
            v = s_in[g] if step == 0 else s[g]
            v = v + C[0, g] + C[1, g] * f
            v = v + C[4, g] * F[g, first + 1 : first + 1 + EXT] + C[5, g] * F[g, first - 1 : first - 1 + EXT]
            v = v + C[2, g] * to_next(ups, g) + C[3, g] * to_prev(downs, g)
            v = v + C[6, g] * roll(f, -1, 1) + C[7, g] * roll(f, 1, 1)
            s[g] = v
    for g in (1, 2):
        put(s[g, 0:NYL, :], g, s_nat)
    s_copy = pltpu.make_async_copy(s_nat, s_out, sem.at[1])
    s_copy.start()
    np_copy.wait()
    s_copy.wait()


def solution(mesh):
    n_gx, n_gy = mesh.shape["gx"], mesh.shape["gy"]
    vmem = pl.BlockSpec(memory_space=pltpu.VMEM)
    anywhere = pl.BlockSpec(memory_space=pltpu.HBM)

    def body(perm, facies, fpor, fmob, pressure, saturation, basis, bx_map, by_map, well_cells, well_rates):
        assert pressure.shape == (NZ, NXL, NYL) and n_gx % 2 == 0
        flat = [a.reshape(NZ * NXL, NYL) for a in (perm, facies, pressure, saturation, basis)]
        sizes = (n_gx, n_gy, by_map.shape[0])
        wide = pltpu.VMEM((GROUPS, EXT, 128), f32)
        cells_in = lambda kind=f32: pltpu.VMEM((NZ * NXL, NYL), kind)
        natural = [cells_in(), cells_in(jnp.int32), cells_in(), cells_in(), cells_in()]
        facies_tables = [pltpu.SMEM(fpor.shape, f32), pltpu.SMEM(fmob.shape, f32)]
        in_vmem = lambda v: pltpu.with_memory_space_constraint(v, pltpu.VMEM)
        in_hbm = lambda v: pltpu.with_memory_space_constraint(v, pltpu.HBM)
        block = pltpu.VMEM((5, NYL, 128), f32)
        edge = pltpu.VMEM((3 * NZ, NYL), f32)
        link = pl.pallas_call(
            lambda *refs: pair_kernel(n_gx, *refs),
            name="link",
            out_shape=[block, edge],
            in_specs=[anywhere] * 7,
            out_specs=[vmem] * 2,
            scratch_shapes=natural + facies_tables + [
                pltpu.SemaphoreType.DMA((7,)),
                cells_in(), cells_in(),
                block, edge, block, edge,
                pltpu.SemaphoreType.DMA((2,)),
                pltpu.SemaphoreType.DMA((2,)),
            ],
            compiler_params=pltpu.CompilerParams(collective_id=1, has_side_effects=True, vmem_limit_bytes=16 << 20),
        )(*[in_hbm(v) for v in (*flat, fpor, fmob)])
        results = pl.pallas_call(
            lambda *refs: comm_kernel(sizes, *refs),
            name="exchange",
            out_shape=[wide] * 7,
            in_specs=[vmem] * 7 + [anywhere] * 6,
            out_specs=[vmem] * 7,
            scratch_shapes=[
                pltpu.VMEM((n_gy, NYL), jnp.int32),
                pltpu.VMEM((1, well_cells.shape[0]), jnp.int32),
                pltpu.VMEM((1, well_cells.shape[0]), f32),
                pltpu.SMEM(bx_map.shape, jnp.int32),
            ] + facies_tables + [
                pltpu.SemaphoreType.DMA((6,)),
                cells_in(), cells_in(),
                pltpu.VMEM((5, GROUPS, EXT, 128), f32),
                pltpu.VMEM((2, 5, GROUPS, 8, 128), f32),
                edge, edge,
                pltpu.VMEM((2, 8, 128), f32),
                pltpu.VMEM((2, 8, 128), f32),
                pltpu.VMEM((2 * REACH + 1, ROWS_C, 128), f32),
                pltpu.VMEM((2 * REACH + 1, 8, 128), f32),
                pltpu.VMEM((2 * REACH + 1, 8, 128), f32),
                pltpu.SemaphoreType.DMA((4,)),
                pltpu.SemaphoreType.DMA((4,)),
                pltpu.SemaphoreType.DMA((10,)),
                pltpu.SemaphoreType.DMA((10,)),
                pltpu.SemaphoreType.DMA((27,)),
                pltpu.SemaphoreType.DMA((27,)),
            ],
            compiler_params=pltpu.CompilerParams(collective_id=0, has_side_effects=True, vmem_limit_bytes=32 << 20),
        )(
            *[in_vmem(v) for v in flat], *[in_vmem(v) for v in link],
            *[in_hbm(v) for v in (by_map.reshape(n_gy, NYL), well_cells.reshape(1, -1), well_rates.reshape(1, -1), bx_map)],
            fpor, fmob,
        )
        shape = jax.ShapeDtypeStruct((NZ * NXL, NYL), f32)
        new_pressure, water = pl.pallas_call(
            transport_kernel,
            name="transport",
            out_shape=[shape, shape],
            in_specs=[vmem] * 7,
            out_specs=[anywhere] * 2,
            scratch_shapes=[
                pltpu.VMEM((GROUPS, EXT, 128), f32),
                pltpu.VMEM((GROUPS, EXT + 16, 128), f32),
                pltpu.VMEM((8, GROUPS, EXT, 128), f32),
                cells_in(), cells_in(),
                pltpu.SemaphoreType.DMA((2,)),
            ],
            compiler_params=pltpu.CompilerParams(vmem_limit_bytes=32 << 20),
        )(*[in_vmem(v) for v in results])
        return new_pressure.reshape(pressure.shape), water.reshape(pressure.shape)

    cells = P("member", "gx", "gy")
    return jax.shard_map(
        body,
        mesh=mesh,
        in_specs=(cells, cells, P(), P(), cells, cells, cells, P("member"), P("member"), P("member"), P("member")),
        out_specs=(cells, cells),
        check_vma=False,
    )
```

time: 57.3 us -> 57.3 us (level)
  Pallas kernels: 56.6 us -> 55.8 us
  local copies, waits for them, and re-layouts: 0 us -> 0.63 us
    pallas_call x1, Pallas kernels: 53.5 us -> 42.6 us  [body(): pl.pallas_call(lambda *refs: comm_kernel(sizes, *refs), name='exchange',...]
    pallas_call x0 -> x1, Pallas kernels: none -> 10.4 us  [body(): pl.pallas_call(lambda *refs: pair_kernel(n_gx, *refs), name='link', out_s...]
    unnamed x0 -> x14, local copies, waits for them, and re-layouts: none -> 0.63 us
where the time goes in v3:
time: 57.3 us; the launch traced here: 57.2 us
  Pallas kernels  55.8 us (97%)
  between operations  0.74 us (1%)
  local copies, waits for them, and re-layouts  0.63 us (1%)
    pallas_call x1, Pallas kernels, body(): pl.pallas_call(lambda *refs: comm_kernel(sizes, *refs), name='exchange',...  42.6 us
    pallas_call x1, Pallas kernels, body(): pl.pallas_call(lambda *refs: pair_kernel(n_gx, *refs), name='link', out_s...  10.4 us
    pallas_call x1, Pallas kernels, body(): pl.pallas_call(transport_kernel, name='transport', out_shape=[shape, shap...  2.88 us

profile of v3, /device:TPU:65, one launch (start us, length us, event | category | flops | bytes accessed | tf_op | source)
XLA Modules:
  0.0 57.2 jit_solution(2493370028228882843)
XLA Ops:
  0.6 0.0 copy-start
  0.6 0.0 copy-start.1
  0.7 0.0 copy-start.2
  0.7 0.0 copy-start.3
  0.7 0.0 copy-start.4
  0.7 10.4 %link.1 = (f32[5,128,128]{2,1,0:T(8,128)S(1)}, f32[96,128]{1,0:T(8,128)S(1)}) custom-call(f32[256,128]{1,0:T(8,128)} %bitcast.10, s32[256,128]{1,0:T(8,128)} %bitcast.12, f32[256,128]{1,0:T(8,128)} %bitcast.14, f32[256,128]{1,0:T(8,128)} %bitcast.16, f32[256,128]{1,0:T(8,128)} %bitcast.18, f32[4]{0:T(128)} %refs_11_.1, f32[4]{0:T(128)} %refs_12_.1), custom_call_target="tpu_custom_call" | custom-call | tf_op jit(solution)/shard_map/link/pallas_call | solution.py:592
  11.1 0.0 copy-start.5
  11.1 0.0 copy-start.6
  11.1 0.0 copy-done
  11.1 0.0 copy-done.1
  11.1 0.0 copy-done.2
  11.1 0.0 copy-done.3
  11.1 0.0 copy-done.4
  11.1 0.6 %copy-done.5 = f32[4]{0:T(128)S(1)} copy-done((f32[4]{0:T(128)S(1)}, f32[4]{0:T(128)}, u32[]{:S(2)}) %copy-start.5) | copy-done | bytes 40
  11.7 0.0 copy-done.6
  11.7 42.6 %exchange.1 = (f32[4,136,128]{2,1,0:T(8,128)S(1)}, f32[4,136,128]{2,1,0:T(8,128)S(1)}, f32[4,136,128]{2,1,0:T(8,128)S(1)}, f32[4,136,128]{2,1,0:T(8,128)S(1)}, f...) custom-call(f32[256,128]{1,0:T(8,128)S(1)} %bitcast.11, ...), custom_call_target="tpu_custom_call" | custom-call | tf_op jit(solution)/shard_map/exchange/pallas_call | solution.py:607
  54.3 2.9 %transport.1 = (f32[256,128]{1,0:T(8,128)}, f32[256,128]{1,0:T(8,128)}) custom-call(f32[4,136,128]{2,1,0:T(8,128)S(1)} %get-tuple-element.15.tx, f32[4,136,128]{2,1,0:T(8,128)S(1)} %get-tuple-element.16.ty, f32[4,136,128]{2,1,0:T(8,128)S(1)} %get-tuple-element.17.tz, f32[4,136,128]{2,1,0:T(8,128)S(1)} %get-tuple-element.18.s_in, ...), custom_call_target="tpu_custom_call" | custom-call | tf_op jit(solution)/shard_map/transport/pallas_call | solution.py:643
Async XLA Ops:
  0.6 10.4 %copy-start = (f32[32,8,128]{2,1,0:T(8,128)S(1)}, f32[32,8,128]{2,1,0:T(8,128)}, u32[]{:S(2)}) copy-start(f32[32,8,128]{2,1,0:T(8,128)} %param.11) | copy-start | bytes 393220
  0.6 10.4 %copy-start.1 = (s32[32,8,128]{2,1,0:T(8,128)S(1)}, s32[32,8,128]{2,1,0:T(8,128)}, u32[]{:S(2)}) copy-start(s32[32,8,128]{2,1,0:T(8,128)} %param.12) | copy-start | bytes 393220
  0.7 10.4 %copy-start.2 = (f32[32,8,128]{2,1,0:T(8,128)S(1)}, f32[32,8,128]{2,1,0:T(8,128)}, u32[]{:S(2)}) copy-start(f32[32,8,128]{2,1,0:T(8,128)} %param.15) | copy-start | bytes 393220
  0.7 10.4 %copy-start.3 = (f32[32,8,128]{2,1,0:T(8,128)S(1)}, f32[32,8,128]{2,1,0:T(8,128)}, u32[]{:S(2)}) copy-start(f32[32,8,128]{2,1,0:T(8,128)} %param.16) | copy-start | bytes 393220
  0.7 10.4 %copy-start.4 = (f32[32,8,128]{2,1,0:T(8,128)S(1)}, f32[32,8,128]{2,1,0:T(8,128)}, u32[]{:S(2)}) copy-start(f32[32,8,128]{2,1,0:T(8,128)} %param.17) | copy-start | bytes 393220
  11.1 0.7 %copy-start.5 = (f32[4]{0:T(128)S(1)}, f32[4]{0:T(128)}, u32[]{:S(2)}) copy-start(f32[4]{0:T(128)} %refs_11_.1) | copy-start | bytes 52
  11.1 0.7 %copy-start.6 = (f32[4]{0:T(128)S(1)}, f32[4]{0:T(128)}, u32[]{:S(2)}) copy-start(f32[4]{0:T(128)} %refs_12_.1) | copy-start | bytes 52

commit v4 on v3

--- a/solution.py
+++ b/solution.py
@@ -18,11 +18,12 @@
 GROUPS = 4
 ROWS_C = 24
 REACH = 4
+CHUNK = 16
 
 time_step = 0.005
 f32 = jnp.float32
 bf16 = jnp.bfloat16
-M, PR, B, S, PHI = range(5)
+M, PR, B, PHI, S = range(5)
 
 
 def iota(shape, dim):
@@ -106,73 +107,17 @@
         pl.when(self.comes)(lambda: self.copy.wait_recv())
 
 
-def pair_kernel(
-    n_gx, perm_h, fac_h, pres_h, sat_h, bas_h, fpor_h, fmob_h, block_out, edge_out,
-    perm, fac, pres, sat, bas, fpor, fmob, in_sem, mob, por, block, edge, block_in, edge_in, send, recv,
-):
-    gx = lax.axis_index("gx")
-    odd = gx % 2 == 1
-    partner = jnp.where(odd, gx + 1, gx - 1)
-    linked = (partner >= 0) & (partner < n_gx)
-    barrier = pltpu.get_barrier_semaphore()
-
-    @pl.when(jnp.logical_not(linked))
-    def _():
-        block_out[...] = jnp.zeros_like(block_out)
-        edge_out[...] = jnp.zeros_like(edge_out)
-
-    @pl.when(linked)
-    def _():
-        inputs = [
-            pltpu.make_async_copy(src, dst, in_sem.at[i])
-            for i, (src, dst) in enumerate(zip(
-                (sat_h, fac_h, perm_h, fpor_h, fmob_h, pres_h, bas_h), (sat, fac, perm, fpor, fmob, pres, bas)
-            ))
-        ]
-        for copy in inputs:
-            copy.start()
-        pl.semaphore_signal(barrier, inc=1, device_id={"gx": partner}, device_id_type=pl.DeviceIdType.MESH)
-        for copy in inputs:
-            copy.wait()
-        fetch_properties(perm, fac, sat, fpor, fmob, mob, por)
-
-        def fill(g, x):
-            for f, ref in ((M, mob), (PR, pres), (B, bas), (S, sat), (PHI, por)):
-                block[f] = turned(ref, g)
-            for k, ref in enumerate((mob, pres, bas)):
-                edge[NZ * k : NZ * (k + 1)] = edge_rows(ref, x)
-
-        pl.when(odd)(lambda: fill(2, NXL - 1))
-        pl.when(jnp.logical_not(odd))(lambda: fill(1, 0))
-        pl.semaphore_wait(barrier, 1)
-        copies = [
-            pltpu.make_async_remote_copy(
-                src_ref=src, dst_ref=dst, send_sem=send.at[i], recv_sem=recv.at[i],
-                device_id={"gx": partner}, device_id_type=pl.DeviceIdType.MESH,
-            )
-            for i, (src, dst) in enumerate(((edge, edge_in), (block, block_in)))
-        ]
-        for copy in copies:
-            copy.start()
-        for copy in copies:
-            copy.wait()
-        block_out[...] = block_in[...]
-        edge_out[...] = edge_in[...]
-
-
 def comm_kernel(
     sizes,
-    perm, fac, pres, sat, bas, block_in, edge_in, bymap_h, wells_h, rates_h, bxmap_h, fpor_h, fmob_h,
+    perm_h, fac_h, pres_h, sat_h, bas_h, bymap_h, wells_h, rates_h, bxmap_h, fpor_h, fmob_h,
     tx_out, ty_out, tz_out, s_out, w_out, src_out, newp,
-    bymap, wells, rates, bxmap, fpor, fmob, in_sem,
+    perm, fac, pres, sat, bas, bymap, wells, rates, bxmap, fpor, fmob, in_sem,
     mob, por, E, yh, xs, xr, ys, yr, ps, low, high,
     send_a, recv_a, send_h, recv_h, send_c, recv_c,
 ):
     n_gx, n_gy, full_y = sizes
     gx = lax.axis_index("gx")
     gy = lax.axis_index("gy")
-    odd = gx % 2 == 1
-    even = jnp.logical_not(odd)
 
     def there(dx, dy):
         ok = jnp.bool_(True)
@@ -186,26 +131,17 @@
         return {"gx": gx + dx, "gy": gy + dy}
 
     partners = [(dx, dy) for dx in range(-REACH, REACH + 1) for dy in (-1, 0, 1) if (dx, dy) != (0, 0)]
-    partners.sort(key=lambda d: abs(d[0]) + abs(d[1]))
+    partners.sort(key=lambda d: -abs(d[0]) - abs(d[1]))
 
     inputs = [
         pltpu.make_async_copy(src, dst, in_sem.at[i])
         for i, (src, dst) in enumerate(zip(
-            (fpor_h, fmob_h, bxmap_h, bymap_h, wells_h, rates_h), (fpor, fmob, bxmap, bymap, wells, rates)
+            (sat_h, fac_h, perm_h, fpor_h, fmob_h, pres_h, bas_h, bxmap_h, bymap_h, wells_h, rates_h),
+            (sat, fac, perm, fpor, fmob, pres, bas, bxmap, bymap, wells, rates),
         ))
     ]
     for copy in inputs:
         copy.start()
-
-    at_edge = (gx < REACH) | (gx >= n_gx - REACH) | (gy == 0) | (gy == n_gy - 1)
-
-    @pl.when(at_edge)
-    def _():
-        ps[...] = jnp.zeros_like(ps)
-        low[...] = jnp.zeros_like(low)
-        high[...] = jnp.zeros_like(high)
-        yh[...] = jnp.zeros_like(yh)
-        yr[...] = jnp.zeros_like(yr)
 
     barrier = pltpu.get_barrier_semaphore()
     for dx, dy in partners:
@@ -213,9 +149,11 @@
         def _(dx=dx, dy=dy):
             pl.semaphore_signal(barrier, inc=1, device_id=where_is(dx, dy), device_id_type=pl.DeviceIdType.MESH)
 
-    for copy in inputs[:2]:
+    for copy in inputs[:5]:
         copy.wait()
     fetch_properties(perm, fac, sat, fpor, fmob, mob, por)
+    for copy in inputs[5:7]:
+        copy.wait()
 
     def turn(pairs):
         for f, ref in pairs:
@@ -231,8 +169,9 @@
     own_edge = []
     for x in (0, NXL - 1):
         own_edge.append([edge_rows(ref, x) for ref in (mob, pres, bas)])
-    for k in range(3):
-        xs[NZ * k : NZ * (k + 1)] = jnp.where(odd, own_edge[0][k], own_edge[1][k])
+    for side in (0, 1):
+        for k in range(3):
+            xs[side, NZ * k : NZ * (k + 1)] = own_edge[side][k]
 
     span_x = lax.min(gx, REACH) + lax.min(n_gx - 1 - gx, REACH) + 1
     span_y = lax.min(gy, 1) + lax.min(n_gy - 1 - gy, 1) + 1
@@ -241,16 +180,15 @@
     def to(src, dst, sends, recvs, slot_out, slot_in, dx, dy):
         return Copy(src, dst, sends.at[slot_out], recvs.at[slot_in], where_is(dx, dy), there(dx, dy), there(-dx, -dy))
 
-    mate = {"gx": jnp.where(odd, gx - 1, gx + 1)}
-    always = jnp.bool_(True)
     edges = [
         to(ys.at[1], yr.at[0], send_a, recv_a, 2, 2, 0, 1),
         to(ys.at[0], yr.at[1], send_a, recv_a, 3, 3, 0, -1),
-        Copy(xs, xr, send_a.at[0], recv_a.at[0], mate, always, always),
+        to(xs.at[1], xr.at[0], send_a, recv_a, 0, 0, 1, 0),
+        to(xs.at[0], xr.at[1], send_a, recv_a, 1, 1, -1, 0),
     ]
     for copy in edges:
         copy.start()
-    turn(((S, sat), (PHI, por)))
+    turn(((PHI, por),))
 
     up, down = slice(NYL - 8, NYL), slice(0, 8)
     every = slice(0, 5)
@@ -261,21 +199,38 @@
         to(E.at[every, 1, up], yh.at[0, every, 3], send_h, recv_h, 7, 7, -1, 1),
         to(E.at[every, 2, down], yh.at[1, every, 0], send_h, recv_h, 8, 8, 1, -1),
         to(E.at[every, 1, down], yh.at[1, every, 3], send_h, recv_h, 9, 9, -1, -1),
-        Copy(E.at[every, 2, 0:NYL], E.at[every, 0, 0:NYL], send_h.at[0], recv_h.at[0], mate, even, odd),
-        Copy(E.at[every, 1, 0:NYL], E.at[every, 3, 0:NYL], send_h.at[1], recv_h.at[1], mate, odd, even),
     ]
+
+    def halo_x(k, fields):
+        return [
+            to(E.at[fields, 2, 0:NYL], E.at[fields, 0, 0:NYL], send_h, recv_h, 2 * k, 2 * k, 1, 0),
+            to(E.at[fields, 1, 0:NYL], E.at[fields, 3, 0:NYL], send_h, recv_h, 2 * k + 1, 2 * k + 1, -1, 0),
+        ]
+
+    halo_early = halo_x(0, slice(0, 4))
+    halo_late = halo_x(1, slice(4, 5))
+    for copy in halo_early:
+        copy.start()
+    turn(((S, sat),))
     for copy in halo:
         copy.start()
-    for copy in inputs[2:]:
+    for copy in inputs[7:]:
         copy.wait()
 
-    @pl.when(even)
-    def _():
-        E[every, 0, 0:NYL] = block_in[...]
-
-    @pl.when(odd)
-    def _():
-        E[every, 3, 0:NYL] = block_in[...]
+    def clear_if(missing, *parts):
+        @pl.when(missing)
+        def _():
+            for ref, where in parts:
+                ref[where] = jnp.zeros(ref.at[where].shape, f32)
+
+    whole = slice(None)
+    clear_if(gx == 0, (xr, 0), (E, (whole, 0)), (yh, (whole, whole, 0)))
+    clear_if(gx == n_gx - 1, (xr, 1), (E, (whole, 3)), (yh, (whole, whole, 3)))
+    clear_if(gy == 0, (yr, 0), (yh, 0), (low, whole))
+    clear_if(gy == n_gy - 1, (yr, 1), (yh, 1), (high, whole))
+    for dx in range(1, REACH + 1):
+        for k, missing in ((REACH - dx, gx - dx < 0), (REACH + dx, gx + dx >= n_gx)):
+            clear_if(missing, (ps, k), (low, k), (high, k))
 
     well_y = wells[...] % full_y
     well_x = wells[...] // full_y
@@ -373,10 +328,8 @@
     for copy in edges:
         copy.wait_recv()
 
-    from_mate = [xr[NZ * k : NZ * (k + 1)] for k in range(3)]
-    from_link = [edge_in[NZ * k : NZ * (k + 1)] for k in range(3)]
-    m0, p0, b0 = [jnp.where(odd, v, w) for v, w in zip(from_mate, from_link)]
-    m1, p1, b1 = [jnp.where(odd, w, v) for v, w in zip(from_mate, from_link)]
+    m0, p0, b0 = [xr[0, NZ * k : NZ * (k + 1)] for k in range(3)]
+    m1, p1, b1 = [xr[1, NZ * k : NZ * (k + 1)] for k in range(3)]
     (om0, op0, ob0), (om1, op1, ob1) = own_edge
     t1 = harmonic(om1, m1)
     t0 = harmonic(om0, m0)
@@ -443,12 +396,14 @@
         for dy in (1, -1, 0):
             if (dx, dy) in coarse:
                 coarse[dx, dy].start()
+    for copy in halo_late:
+        copy.start()
 
     target = (lanes_of(kx, (1, 512)) + 3) * 8 + (iota((1, 512), 1) % NZ) // BZ
     spread_xz = (iota((64, 512), 0) == target).astype(f32).astype(bf16)
     spread_xz = jnp.concatenate([spread_xz] * 3, axis=0)
 
-    for copy in halo:
+    for copy in halo_early + halo:
         copy.wait_recv()
     take_up = iota((8, 128), 0) < 4
     for f in range(5):
@@ -462,13 +417,17 @@
         tx_out[g] = harmonic(here, next_x(here, E[M, after]))
         ty_out[g] = harmonic(here, roll(here, -1, 0))
         tz_out[g] = jnp.where(z_ext < NZ - 1, 0.1 * harmonic(here, roll(here, -1, 1)), 0.0)
-        s_out[g] = E[S, g]
         phi_here = E[PHI, g]
         w_out[g] = time_step / jnp.where(phi_here > 0, phi_here, 1.0)
 
     lane24 = iota((ROWS_C, 128), 1)
     system = [jnp.zeros((ROWS_C, 128), f32) for _ in range(5)]
     for dx in sorted(range(-REACH, REACH + 1), key=abs):
+        if dx == REACH - 1:
+            for copy in halo_late:
+                copy.wait_recv()
+            for g in range(GROUPS):
+                s_out[g] = E[S, g]
         for dy in (-1, 0, 1):
             if (dx, dy) in coarse:
                 coarse[-dx, -dy].wait_recv()
@@ -476,7 +435,7 @@
         part = jnp.concatenate([ps[k, 0:8] + low[k], ps[k, 8:16], ps[k, 16:24] + high[k]], axis=0)
         first = (dx + 2) * 8
         take = (lane24 >= max(first, 0)) & (lane24 < min(first + 24, 56))
-        for q in range(5):
+        for q in range(2 if abs(dx) == REACH else 5):
             system[q] = system[q] + jnp.where(take, roll(part, first - 24 * q, 1), 0.0)
     resid, diag, cz, cx, cy = system
     diag = jnp.where(diag > 0, diag, 1.0)
@@ -498,7 +457,7 @@
 
     for g in range(GROUPS):
         newp[g] = E[PR, g] + E[B, g] * fine[:, 128 * g : 128 * (g + 1)]
-    for copy in edges + halo + list(coarse.values()):
+    for copy in edges + halo + halo_early + halo_late + list(coarse.values()):
         copy.wait_send()
 
 
@@ -548,22 +507,29 @@
     for step in range(NSUB):
         last = step == NSUB - 1
         for g in range(GROUPS):
-            v = s_in[g] if step == 0 else s[g]
-            wet = v * v
-            f = wet / (wet + (1.0 - v) * (1.0 - v) * 0.25)
-            F[g, first : first + EXT] = f
-            F[g, first - 1 : first] = f[EXT - 1 : EXT]
-            F[g, last_row + 1 : last_row + 2] = f[0:1]
-        ups = [roll(F[g, first : first + EXT], -32, 1) if g or not last else None for g in range(GROUPS)]
-        downs = [roll(F[g, first : first + EXT], 32, 1) if g < 3 or not last else None for g in range(GROUPS)]
-        for g in (1, 2) if last else range(GROUPS):
-            f = F[g, first : first + EXT]
-            v = s_in[g] if step == 0 else s[g]
-            v = v + C[0, g] + C[1, g] * f
-            v = v + C[4, g] * F[g, first + 1 : first + 1 + EXT] + C[5, g] * F[g, first - 1 : first - 1 + EXT]
-            v = v + C[2, g] * to_next(ups, g) + C[3, g] * to_prev(downs, g)
-            v = v + C[6, g] * roll(f, -1, 1) + C[7, g] * roll(f, 1, 1)
-            s[g] = v
+            for a in range(0, EXT, CHUNK):
+                b = min(a + CHUNK, EXT)
+                v = s_in[g, a:b] if step == 0 else s[g, a:b]
+                wet = v * v
+                F[g, first + a : first + b] = wet / (wet + (1.0 - v) * (1.0 - v) * 0.25)
+            F[g, first - 1 : first] = F[g, last_row : last_row + 1]
+            F[g, last_row + 1 : last_row + 2] = F[g, first : first + 1]
+        end = NYL if last else EXT
+        for a in range(0, end, CHUNK):
+            b = min(a + CHUNK, end)
+            here = [F[g, first + a : first + b] for g in range(GROUPS)]
+            mask_next, mask_prev = lane[a:b] < 96, lane[a:b] >= 32
+            ups = [None if last and g == 0 else roll(f, -32, 1) for g, f in enumerate(here)]
+            downs = [None if last and g == 3 else roll(f, 32, 1) for g, f in enumerate(here)]
+            for g in (1, 2) if last else range(GROUPS):
+                v = s_in[g, a:b] if step == 0 else s[g, a:b]
+                v = v + C[0, g, a:b] + C[1, g, a:b] * here[g]
+                v = v + C[4, g, a:b] * F[g, first + a + 1 : first + b + 1]
+                v = v + C[5, g, a:b] * F[g, first + a - 1 : first + b - 1]
+                v = v + C[2, g, a:b] * jnp.where(mask_next, ups[g], ups[min(g + 1, GROUPS - 1)])
+                v = v + C[3, g, a:b] * jnp.where(mask_prev, downs[g], downs[max(g - 1, 0)])
+                v = v + C[6, g, a:b] * roll(here[g], -1, 1) + C[7, g, a:b] * roll(here[g], 1, 1)
+                s[g, a:b] = v
     for g in (1, 2):
         put(s[g, 0:NYL, :], g, s_nat)
     s_copy = pltpu.make_async_copy(s_nat, s_out, sem.at[1])
@@ -578,7 +544,7 @@
     anywhere = pl.BlockSpec(memory_space=pltpu.HBM)
 
     def body(perm, facies, fpor, fmob, pressure, saturation, basis, bx_map, by_map, well_cells, well_rates):
-        assert pressure.shape == (NZ, NXL, NYL) and n_gx % 2 == 0
+        assert pressure.shape == (NZ, NXL, NYL)
         flat = [a.reshape(NZ * NXL, NYL) for a in (perm, facies, pressure, saturation, basis)]
         sizes = (n_gx, n_gy, by_map.shape[0])
         wide = pltpu.VMEM((GROUPS, EXT, 128), f32)
@@ -587,36 +553,20 @@
         facies_tables = [pltpu.SMEM(fpor.shape, f32), pltpu.SMEM(fmob.shape, f32)]
         in_vmem = lambda v: pltpu.with_memory_space_constraint(v, pltpu.VMEM)
         in_hbm = lambda v: pltpu.with_memory_space_constraint(v, pltpu.HBM)
-        block = pltpu.VMEM((5, NYL, 128), f32)
-        edge = pltpu.VMEM((3 * NZ, NYL), f32)
-        link = pl.pallas_call(
-            lambda *refs: pair_kernel(n_gx, *refs),
-            name="link",
-            out_shape=[block, edge],
-            in_specs=[anywhere] * 7,
-            out_specs=[vmem] * 2,
-            scratch_shapes=natural + facies_tables + [
-                pltpu.SemaphoreType.DMA((7,)),
-                cells_in(), cells_in(),
-                block, edge, block, edge,
-                pltpu.SemaphoreType.DMA((2,)),
-                pltpu.SemaphoreType.DMA((2,)),
-            ],
-            compiler_params=pltpu.CompilerParams(collective_id=1, has_side_effects=True, vmem_limit_bytes=16 << 20),
-        )(*[in_hbm(v) for v in (*flat, fpor, fmob)])
+        edge = pltpu.VMEM((2, 3 * NZ, NYL), f32)
         results = pl.pallas_call(
             lambda *refs: comm_kernel(sizes, *refs),
             name="exchange",
             out_shape=[wide] * 7,
-            in_specs=[vmem] * 7 + [anywhere] * 6,
+            in_specs=[anywhere] * 11,
             out_specs=[vmem] * 7,
-            scratch_shapes=[
+            scratch_shapes=natural + [
                 pltpu.VMEM((n_gy, NYL), jnp.int32),
                 pltpu.VMEM((1, well_cells.shape[0]), jnp.int32),
                 pltpu.VMEM((1, well_cells.shape[0]), f32),
                 pltpu.SMEM(bx_map.shape, jnp.int32),
             ] + facies_tables + [
-                pltpu.SemaphoreType.DMA((6,)),
+                pltpu.SemaphoreType.DMA((11,)),
                 cells_in(), cells_in(),
                 pltpu.VMEM((5, GROUPS, EXT, 128), f32),
                 pltpu.VMEM((2, 5, GROUPS, 8, 128), f32),
@@ -635,9 +585,9 @@
             ],
             compiler_params=pltpu.CompilerParams(collective_id=0, has_side_effects=True, vmem_limit_bytes=32 << 20),
         )(
-            *[in_vmem(v) for v in flat], *[in_vmem(v) for v in link],
-            *[in_hbm(v) for v in (by_map.reshape(n_gy, NYL), well_cells.reshape(1, -1), well_rates.reshape(1, -1), bx_map)],
-            fpor, fmob,
+            *[in_hbm(v) for v in (
+                *flat, by_map.reshape(n_gy, NYL), well_cells.reshape(1, -1), well_rates.reshape(1, -1), bx_map, fpor, fmob
+            )]
         )
         shape = jax.ShapeDtypeStruct((NZ * NXL, NYL), f32)
         new_pressure, water = pl.pallas_call(

time: 57.3 us -> 55.7 us (0.972)
  Pallas kernels: 55.8 us -> 55 us
  local copies, waits for them, and re-layouts: 0.63 us -> 0 us
    pallas_call x1 -> x0, Pallas kernels: 10.4 us -> none  [body(): pl.pallas_call(lambda *refs: pair_kernel(n_gx, *refs), name='link', out_s...]
    pallas_call x1, Pallas kernels: 42.6 us -> 52.5 us  [body(): pl.pallas_call(lambda *refs: comm_kernel(sizes, *refs), name='exchange',...]
    unnamed x14 -> x0, local copies, waits for them, and re-layouts: 0.63 us -> none
where the time goes in v4:
time: 55.7 us; the launch traced here: 55.6 us
  Pallas kernels  55 us (99%)
  between operations  0.64 us (1%)
    pallas_call x1, Pallas kernels, body(): pl.pallas_call(lambda *refs: comm_kernel(sizes, *refs), name='exchange',...  52.5 us
    pallas_call x1, Pallas kernels, body(): pl.pallas_call(transport_kernel, name='transport', out_shape=[shape, shap...  2.46 us

profile of v4, /device:TPU:65, one launch (start us, length us, event | category | flops | bytes accessed | tf_op | source)
XLA Modules:
  0.0 55.6 jit_solution(15763605407056460332)
XLA Ops:
  0.6 52.5 %exchange.1 = (f32[4,136,128]{2,1,0:T(8,128)S(1)}, f32[4,136,128]{2,1,0:T(8,128)S(1)}, f32[4,136,128]{2,1,0:T(8,128)S(1)}, f32[4,136,128]{2,1,0:T(8,128)S(1)}, f...) custom-call(f32[256,128]{1,0:T(8,128)} %bitcast.10, s32[256,128]{1,0:T(8,128)} %bitcast.11, ...), custom_call_target="tpu_custom_call" | custom-call | tf_op jit(solution)/shard_map/exchange/pallas_call | solution.py:557
  53.1 2.5 %transport.1 = (f32[256,128]{1,0:T(8,128)}, f32[256,128]{1,0:T(8,128)}) custom-call(f32[4,136,128]{2,1,0:T(8,128)S(1)} %get-tuple-element.11.tx, f32[4,136,128]{2,1,0:T(8,128)S(1)} %get-tuple-element.12.ty, f32[4,136,128]{2,1,0:T(8,128)S(1)} %get-tuple-element.13.tz, f32[4,136,128]{2,1,0:T(8,128)S(1)} %get-tuple-element.14.s_in, ...), custom_call_target="tpu_custom_call" | custom-call | tf_op jit(solution)/shard_map/transport/pallas_call | solution.py:593

commit v5 on v4

--- a/solution.py
+++ b/solution.py
@@ -131,7 +131,7 @@
         return {"gx": gx + dx, "gy": gy + dy}
 
     partners = [(dx, dy) for dx in range(-REACH, REACH + 1) for dy in (-1, 0, 1) if (dx, dy) != (0, 0)]
-    partners.sort(key=lambda d: -abs(d[0]) - abs(d[1]))
+    partners.sort(key=lambda d: (0, abs(d[0]) + 2 * abs(d[1])) if abs(d[0]) + 2 * abs(d[1]) < 4 else (1, -abs(d[0]) - abs(d[1])))
 
     inputs = [
         pltpu.make_async_copy(src, dst, in_sem.at[i])
@@ -188,7 +188,6 @@
     ]
     for copy in edges:
         copy.start()
-    turn(((PHI, por),))
 
     up, down = slice(NYL - 8, NYL), slice(0, 8)
     every = slice(0, 5)
@@ -207,11 +206,12 @@
             to(E.at[fields, 1, 0:NYL], E.at[fields, 3, 0:NYL], send_h, recv_h, 2 * k + 1, 2 * k + 1, -1, 0),
         ]
 
-    halo_early = halo_x(0, slice(0, 4))
-    halo_late = halo_x(1, slice(4, 5))
-    for copy in halo_early:
+    halo_first = halo_x(0, slice(M, M + 1))
+    halo_next = halo_x(1, slice(PR, B + 1))
+    halo_last = halo_x(5, slice(PHI, S + 1))
+    for copy in halo_first + halo_next:
         copy.start()
-    turn(((S, sat),))
+    turn(((S, sat), (PHI, por)))
     for copy in halo:
         copy.start()
     for copy in inputs[7:]:
@@ -396,14 +396,14 @@
         for dy in (1, -1, 0):
             if (dx, dy) in coarse:
                 coarse[dx, dy].start()
-    for copy in halo_late:
+    for copy in halo_last:
         copy.start()
 
     target = (lanes_of(kx, (1, 512)) + 3) * 8 + (iota((1, 512), 1) % NZ) // BZ
     spread_xz = (iota((64, 512), 0) == target).astype(f32).astype(bf16)
     spread_xz = jnp.concatenate([spread_xz] * 3, axis=0)
 
-    for copy in halo_early + halo:
+    for copy in halo_first + halo:
         copy.wait_recv()
     take_up = iota((8, 128), 0) < 4
     for f in range(5):
@@ -417,17 +417,18 @@
         tx_out[g] = harmonic(here, next_x(here, E[M, after]))
         ty_out[g] = harmonic(here, roll(here, -1, 0))
         tz_out[g] = jnp.where(z_ext < NZ - 1, 0.1 * harmonic(here, roll(here, -1, 1)), 0.0)
+
+    def finish(g):
+        s_out[g] = E[S, g]
         phi_here = E[PHI, g]
         w_out[g] = time_step / jnp.where(phi_here > 0, phi_here, 1.0)
+
+    finish(1)
+    finish(2)
 
     lane24 = iota((ROWS_C, 128), 1)
     system = [jnp.zeros((ROWS_C, 128), f32) for _ in range(5)]
     for dx in sorted(range(-REACH, REACH + 1), key=abs):
-        if dx == REACH - 1:
-            for copy in halo_late:
-                copy.wait_recv()
-            for g in range(GROUPS):
-                s_out[g] = E[S, g]
         for dy in (-1, 0, 1):
             if (dx, dy) in coarse:
                 coarse[-dx, -dy].wait_recv()
@@ -455,9 +456,15 @@
     spread1 = nn(jnp.concatenate(split3(estimate), axis=1), spread_xz)
     fine = nn(jnp.concatenate([spread_y] * 3, axis=1), jnp.concatenate(split3(spread1), axis=0))
 
+    for copy in halo_next:
+        copy.wait_recv()
     for g in range(GROUPS):
         newp[g] = E[PR, g] + E[B, g] * fine[:, 128 * g : 128 * (g + 1)]
-    for copy in edges + halo + halo_early + halo_late + list(coarse.values()):
+    for copy in halo_last:
+        copy.wait_recv()
+    finish(0)
+    finish(3)
+    for copy in edges + halo + halo_first + halo_next + halo_last + list(coarse.values()):
         copy.wait_send()
 
 
@@ -578,8 +585,8 @@
                 pltpu.VMEM((2 * REACH + 1, 8, 128), f32),
                 pltpu.SemaphoreType.DMA((4,)),
                 pltpu.SemaphoreType.DMA((4,)),
-                pltpu.SemaphoreType.DMA((10,)),
-                pltpu.SemaphoreType.DMA((10,)),
+                pltpu.SemaphoreType.DMA((12,)),
+                pltpu.SemaphoreType.DMA((12,)),
                 pltpu.SemaphoreType.DMA((27,)),
                 pltpu.SemaphoreType.DMA((27,)),
             ],

time: 55.7 us -> 55.6 us (level)
  no operation moved by 1% of the time
where the time goes in v5:
time: 55.6 us; the launch traced here: 55.4 us
  Pallas kernels  54.8 us (99%)
  between operations  0.64 us (1%)
    pallas_call x1, Pallas kernels, body(): pl.pallas_call(lambda *refs: comm_kernel(sizes, *refs), name='exchange',...  52.3 us
    pallas_call x1, Pallas kernels, body(): pl.pallas_call(transport_kernel, name='transport', out_shape=[shape, shap...  2.46 us

profile of v5, /device:TPU:65, one launch (start us, length us, event | category | flops | bytes accessed | tf_op | source)
XLA Modules:
  0.0 55.4 jit_solution(3059134303418394677)
XLA Ops:
  0.6 52.3 %exchange.1 = (f32[4,136,128]{2,1,0:T(8,128)S(1)}, f32[4,136,128]{2,1,0:T(8,128)S(1)}, f32[4,136,128]{2,1,0:T(8,128)S(1)}, f32[4,136,128]{2,1,0:T(8,128)S(1)}, f...) custom-call(f32[256,128]{1,0:T(8,128)} %bitcast.10, s32[256,128]{1,0:T(8,128)} %bitcast.11, ...), custom_call_target="tpu_custom_call" | custom-call | tf_op jit(solution)/shard_map/exchange/pallas_call | solution.py:564
  53.0 2.5 %transport.1 = (f32[256,128]{1,0:T(8,128)}, f32[256,128]{1,0:T(8,128)}) custom-call(f32[4,136,128]{2,1,0:T(8,128)S(1)} %get-tuple-element.11.tx, f32[4,136,128]{2,1,0:T(8,128)S(1)} %get-tuple-element.12.ty, f32[4,136,128]{2,1,0:T(8,128)S(1)} %get-tuple-element.13.tz, f32[4,136,128]{2,1,0:T(8,128)S(1)} %get-tuple-element.14.s_in, ...), custom_call_target="tpu_custom_call" | custom-call | tf_op jit(solution)/shard_map/transport/pallas_call | solution.py:600

commit v6 on v5

--- a/solution.py
+++ b/solution.py
@@ -181,10 +181,10 @@
         return Copy(src, dst, sends.at[slot_out], recvs.at[slot_in], where_is(dx, dy), there(dx, dy), there(-dx, -dy))
 
     edges = [
+        to(ys.at[0], yr.at[1], send_a, recv_a, 3, 3, 0, -1),
+        to(xs.at[0], xr.at[1], send_a, recv_a, 1, 1, -1, 0),
         to(ys.at[1], yr.at[0], send_a, recv_a, 2, 2, 0, 1),
-        to(ys.at[0], yr.at[1], send_a, recv_a, 3, 3, 0, -1),
         to(xs.at[1], xr.at[0], send_a, recv_a, 0, 0, 1, 0),
-        to(xs.at[0], xr.at[1], send_a, recv_a, 1, 1, -1, 0),
     ]
     for copy in edges:
         copy.start()
@@ -323,6 +323,16 @@
         hi, mid = split2(jnp.concatenate([sums[0][q], sums[1][q]], axis=1))
         inner.append(nn(sum_y, jnp.concatenate([hi, mid], axis=0)))
 
+    hi, mid = split2(jnp.concatenate(inner, axis=0))
+    partial = nt(jnp.concatenate([hi, mid], axis=1), sum_xz)
+    inside = partial[0:ROWS_C]
+    for q in range(1, 5):
+        inside = inside + roll(partial[ROWS_C * q : ROWS_C * (q + 1)], 24 * q, 1)
+    target = (lanes_of(kx[4:12], (1, 256)) + 1) * 8 + z_block
+    sum_rows = jnp.concatenate(
+        [(iota((128, 256), 0) == target + 24 * q).astype(f32).astype(bf16) for q in (0, 1, 4)] * 2, axis=1
+    )
+
     k_low, k_high, k_next = kx[4], kx[11], kx[12]
     together = k_high == k_next
     for copy in edges:
@@ -367,16 +377,15 @@
     same = r_high == r_next
     couple = ob1 * ub * t1
     zero = jnp.zeros_like(couple)
-    inner[0] = inner[0] + jnp.where(at_high, -ob1 * t1 * (op1 - up_), 0.0) + jnp.where(at_low, -ob0 * t0 * (op0 - dp), 0.0)
-    inner[1] = (
-        inner[1] + jnp.where(at_high, ob1 * ob1 * t1 - 2.0 * jnp.where(same, couple, zero), 0.0)
-        + jnp.where(at_low, ob0 * ob0 * t0, 0.0)
+    at_top = jnp.concatenate(
+        [-ob1 * t1 * (op1 - up_), ob1 * ob1 * t1 - 2.0 * jnp.where(same, couple, zero), jnp.where(same, zero, couple)], axis=1
     )
-    inner[4] = inner[4] + jnp.where(at_high, jnp.where(same, zero, couple), 0.0)
-    hi, mid = split2(jnp.concatenate(inner, axis=0))
-    partial = nt(jnp.concatenate([hi, mid], axis=1), sum_xz)
-    for q in range(5):
-        mine = mine + roll(partial[ROWS_C * q : ROWS_C * (q + 1)], 24 * q, 1)
+    at_bottom = jnp.concatenate([-ob0 * t0 * (op0 - dp), ob0 * ob0 * t0, zero], axis=1)
+    both = jnp.where(iota((8, 768), 0) == 0, at_top, at_bottom)
+    hi, mid = split2(both)
+    edge_y = nt(jnp.concatenate([hi, mid], axis=1), sum_rows)
+    mine = mine + jnp.where(at_high, edge_y[0:1], 0.0) + jnp.where(at_low, edge_y[1:2], 0.0)
+    mine = mine + inside
     ps[REACH] = mine
 
     def slot(dx):
@@ -392,8 +401,8 @@
         coarse[dx, -1] = to(
             ps.at[slot(0), 0:8], high.at[slot(-dx)], send_c, recv_c, 18 + slot(dx), 18 + slot(-dx), dx, -1
         )
-    for dx in (4, -4, 3, -3, 2, -2, 1, -1, 0):
-        for dy in (1, -1, 0):
+    for dx in (-1, -2, -3, -4, 0, 1, 2, 3, 4):
+        for dy in (0, -1, 1):
             if (dx, dy) in coarse:
                 coarse[dx, dy].start()
     for copy in halo_last:
@@ -401,7 +410,7 @@
 
     target = (lanes_of(kx, (1, 512)) + 3) * 8 + (iota((1, 512), 1) % NZ) // BZ
     spread_xz = (iota((64, 512), 0) == target).astype(f32).astype(bf16)
-    spread_xz = jnp.concatenate([spread_xz] * 3, axis=0)
+    spread_xz = jnp.concatenate([spread_xz] * 2, axis=0)
 
     for copy in halo_first + halo:
         copy.wait_recv()
@@ -453,8 +462,8 @@
     row24 = iota((ROWS_C, 128), 0)
     wanted = (row24 >= 3) & (row24 < 21) & (lane24 >= 16) & (lane24 < 40)
     estimate = jnp.where(wanted, estimate, 0.0)[:, 0:64]
-    spread1 = nn(jnp.concatenate(split3(estimate), axis=1), spread_xz)
-    fine = nn(jnp.concatenate([spread_y] * 3, axis=1), jnp.concatenate(split3(spread1), axis=0))
+    spread1 = nn(jnp.concatenate(split2(estimate), axis=1), spread_xz)
+    fine = nn(jnp.concatenate([spread_y] * 2, axis=1), jnp.concatenate(split2(spread1), axis=0))
 
     for copy in halo_next:
         copy.wait_recv()

time: 55.6 us -> 55.3 us (level)
  no operation moved by 1% of the time
where the time goes in v6:
time: 55.3 us; the launch traced here: 55.2 us
  Pallas kernels  54.5 us (99%)
  between operations  0.64 us (1%)
    pallas_call x1, Pallas kernels, body(): pl.pallas_call(lambda *refs: comm_kernel(sizes, *refs), name='exchange',...  52.1 us
    pallas_call x1, Pallas kernels, body(): pl.pallas_call(transport_kernel, name='transport', out_shape=[shape, shap...  2.46 us

profile of v6, /device:TPU:65, one launch (start us, length us, event | category | flops | bytes accessed | tf_op | source)
XLA Modules:
  0.0 55.2 jit_solution(3692186489840280663)
XLA Ops:
  0.6 52.1 %exchange.1 = (f32[4,136,128]{2,1,0:T(8,128)S(1)}, f32[4,136,128]{2,1,0:T(8,128)S(1)}, f32[4,136,128]{2,1,0:T(8,128)S(1)}, f32[4,136,128]{2,1,0:T(8,128)S(1)}, f...) custom-call(f32[256,128]{1,0:T(8,128)} %bitcast.10, s32[256,128]{1,0:T(8,128)} %bitcast.11, ...), custom_call_target="tpu_custom_call" | custom-call | tf_op jit(solution)/shard_map/exchange/pallas_call | solution.py:573
  52.7 2.5 %transport.1 = (f32[256,128]{1,0:T(8,128)}, f32[256,128]{1,0:T(8,128)}) custom-call(f32[4,136,128]{2,1,0:T(8,128)S(1)} %get-tuple-element.11.tx, f32[4,136,128]{2,1,0:T(8,128)S(1)} %get-tuple-element.12.ty, f32[4,136,128]{2,1,0:T(8,128)S(1)} %get-tuple-element.13.tz, f32[4,136,128]{2,1,0:T(8,128)S(1)} %get-tuple-element.14.s_in, ...), custom_call_target="tpu_custom_call" | custom-call | tf_op jit(solution)/shard_map/transport/pallas_call | solution.py:609

commit v7 on v6

--- a/solution.py
+++ b/solution.py
@@ -131,7 +131,7 @@
         return {"gx": gx + dx, "gy": gy + dy}
 
     partners = [(dx, dy) for dx in range(-REACH, REACH + 1) for dy in (-1, 0, 1) if (dx, dy) != (0, 0)]
-    partners.sort(key=lambda d: (0, abs(d[0]) + 2 * abs(d[1])) if abs(d[0]) + 2 * abs(d[1]) < 4 else (1, -abs(d[0]) - abs(d[1])))
+    partners.sort(key=lambda d: -abs(d[0]) - abs(d[1]))
 
     inputs = [
         pltpu.make_async_copy(src, dst, in_sem.at[i])

time: 55.3 us -> 55.1 us (level)
  no operation moved by 1% of the time
where the time goes in v7:
time: 55.1 us; the launch traced here: 55 us
  Pallas kernels  54.3 us (99%)
  between operations  0.64 us (1%)
    pallas_call x1, Pallas kernels, body(): pl.pallas_call(lambda *refs: comm_kernel(sizes, *refs), name='exchange',...  51.9 us
    pallas_call x1, Pallas kernels, body(): pl.pallas_call(transport_kernel, name='transport', out_shape=[shape, shap...  2.46 us

profile of v7, /device:TPU:65, one launch (start us, length us, event | category | flops | bytes accessed | tf_op | source)
XLA Modules:
  0.0 55.0 jit_solution(8516990669298811014)
XLA Ops:
  0.6 51.9 %exchange.1 = (f32[4,136,128]{2,1,0:T(8,128)S(1)}, f32[4,136,128]{2,1,0:T(8,128)S(1)}, f32[4,136,128]{2,1,0:T(8,128)S(1)}, f32[4,136,128]{2,1,0:T(8,128)S(1)}, f...) custom-call(f32[256,128]{1,0:T(8,128)} %bitcast.10, s32[256,128]{1,0:T(8,128)} %bitcast.11, ...), custom_call_target="tpu_custom_call" | custom-call | tf_op jit(solution)/shard_map/exchange/pallas_call | solution.py:573
  52.5 2.5 %transport.1 = (f32[256,128]{1,0:T(8,128)}, f32[256,128]{1,0:T(8,128)}) custom-call(f32[4,136,128]{2,1,0:T(8,128)S(1)} %get-tuple-element.11.tx, f32[4,136,128]{2,1,0:T(8,128)S(1)} %get-tuple-element.12.ty, f32[4,136,128]{2,1,0:T(8,128)S(1)} %get-tuple-element.13.tz, f32[4,136,128]{2,1,0:T(8,128)S(1)} %get-tuple-element.14.s_in, ...), custom_call_target="tpu_custom_call" | custom-call | tf_op jit(solution)/shard_map/transport/pallas_call | solution.py:609

commit v8 on v7

--- a/solution.py
+++ b/solution.py
@@ -401,8 +401,8 @@
         coarse[dx, -1] = to(
             ps.at[slot(0), 0:8], high.at[slot(-dx)], send_c, recv_c, 18 + slot(dx), 18 + slot(-dx), dx, -1
         )
-    for dx in (-1, -2, -3, -4, 0, 1, 2, 3, 4):
-        for dy in (0, -1, 1):
+    for dx in (-3, -2, -4, -1, 0, 1, 2, 3, 4):
+        for dy in (-1, 0, 1):
             if (dx, dy) in coarse:
                 coarse[dx, dy].start()
     for copy in halo_last:
@@ -437,16 +437,18 @@
 
     lane24 = iota((ROWS_C, 128), 1)
     system = [jnp.zeros((ROWS_C, 128), f32) for _ in range(5)]
-    for dx in sorted(range(-REACH, REACH + 1), key=abs):
-        for dy in (-1, 0, 1):
-            if (dx, dy) in coarse:
-                coarse[-dx, -dy].wait_recv()
-        k = slot(dx)
-        part = jnp.concatenate([ps[k, 0:8] + low[k], ps[k, 8:16], ps[k, 16:24] + high[k]], axis=0)
-        first = (dx + 2) * 8
-        take = (lane24 >= max(first, 0)) & (lane24 < min(first + 24, 56))
-        for q in range(2 if abs(dx) == REACH else 5):
-            system[q] = system[q] + jnp.where(take, roll(part, first - 24 * q, 1), 0.0)
+    for group in ((0, -1, 1), (-2, 2), (-3, 3, -4, 4)):
+        for dx in group:
+            for dy in (-1, 0, 1):
+                if (dx, dy) in coarse:
+                    coarse[-dx, -dy].wait_recv()
+        for dx in group:
+            k = slot(dx)
+            part = jnp.concatenate([ps[k, 0:8] + low[k], ps[k, 8:16], ps[k, 16:24] + high[k]], axis=0)
+            first = (dx + 2) * 8
+            take = (lane24 >= max(first, 0)) & (lane24 < min(first + 24, 56))
+            for q in range(2 if abs(dx) == REACH else 5):
+                system[q] = system[q] + jnp.where(take, roll(part, first - 24 * q, 1), 0.0)
     resid, diag, cz, cx, cy = system
     diag = jnp.where(diag > 0, diag, 1.0)
     half = 0.5 / diag

time: 55.1 us -> 55.1 us (level)
  no operation moved by 1% of the time
where the time goes in v8:
time: 55.1 us; the launch traced here: 55 us
  Pallas kernels  54.3 us (99%)
  between operations  0.64 us (1%)
    pallas_call x1, Pallas kernels, body(): pl.pallas_call(lambda *refs: comm_kernel(sizes, *refs), name='exchange',...  51.9 us
    pallas_call x1, Pallas kernels, body(): pl.pallas_call(transport_kernel, name='transport', out_shape=[shape, shap...  2.46 us

profile of v8, /device:TPU:65, one launch (start us, length us, event | category | flops | bytes accessed | tf_op | source)
XLA Modules:
  0.0 55.0 jit_solution(12701328130099314614)
XLA Ops:
  0.6 51.9 %exchange.1 = (f32[4,136,128]{2,1,0:T(8,128)S(1)}, f32[4,136,128]{2,1,0:T(8,128)S(1)}, f32[4,136,128]{2,1,0:T(8,128)S(1)}, f32[4,136,128]{2,1,0:T(8,128)S(1)}, f...) custom-call(f32[256,128]{1,0:T(8,128)} %bitcast.10, s32[256,128]{1,0:T(8,128)} %bitcast.11, ...), custom_call_target="tpu_custom_call" | custom-call | tf_op jit(solution)/shard_map/exchange/pallas_call | solution.py:575
  52.5 2.5 %transport.1 = (f32[256,128]{1,0:T(8,128)}, f32[256,128]{1,0:T(8,128)}) custom-call(f32[4,136,128]{2,1,0:T(8,128)S(1)} %get-tuple-element.11.tx, f32[4,136,128]{2,1,0:T(8,128)S(1)} %get-tuple-element.12.ty, f32[4,136,128]{2,1,0:T(8,128)S(1)} %get-tuple-element.13.tz, f32[4,136,128]{2,1,0:T(8,128)S(1)} %get-tuple-element.14.s_in, ...), custom_call_target="tpu_custom_call" | custom-call | tf_op jit(solution)/shard_map/transport/pallas_call | solution.py:611
